TPU v7x, 32 devices: a whole 2x2x4 slice. The times are simulated.
32 devices in a mesh: grp: 2 (over x), blk: 16 (over z, y, core).
Axes of the slice: x: 2, y: 2, z: 4, core: 2. Of those that a mesh axis runs over, the one named last changes fastest.
Arguments:
- atoms: bfloat16 [16384, 512], P(('grp', 'blk')), parts along dimension 0, may hold values from -8 to 8
- edge_mask: int32 [32, 5, 512, 512], P(('grp', 'blk')), parts along dimension 0, may hold values from 0 to 1
- norm_gain: float32 [512], replicated, may hold values from 0.25 to 1.75
- w_query: bfloat16 [512, 512], replicated, may hold values from -3 to 3
- w_key: bfloat16 [512, 512], replicated, may hold values from -3 to 3
- w_value: bfloat16 [512, 512], replicated, may hold values from -0.25 to 0.25
- w_out: bfloat16 [512, 512], replicated, may hold values from -0.25 to 0.25
- bn_gain: float32 [512], replicated, may hold values from 0.25 to 1.75
- bn_shift: float32 [512], replicated, may hold values from -3 to 3
- w_up: bfloat16 [512, 1024], replicated, may hold values from -0.25 to 0.25
- w_down: bfloat16 [1024, 512], replicated, may hold values from -0.1875 to 0.1875
Outputs:
- updated: bfloat16 [16384, 512], P(('grp', 'blk')), parts along dimension 0
There are 2 independent parts, one for each index of `grp`. A program takes and returns all parts, laid end to end along the dimension named above; an argument that names none is the same for every part. Nothing has to cross between parts.
All inputs are finite; a program needn't handle non-finite values.
Results may differ from a plain program's by a relative error of at most 0.01.
The roundings to bfloat16 on the way count: a program that leaves them out, or rounds other values in their place, can miss the bound.
Values may be sent and summed in bfloat16 or wider, within the bound.
No kernel may reach another device: no remote copies, remote signals or barrier semaphores. Data moves between devices by JAX's collectives and lax.ppermute only.
A program may use at most 128 MiB of HBM per device.

v0:
```python
import functools

import jax
import jax.numpy as jnp
from jax import lax
from jax.experimental import pallas as pl
from jax.experimental.pallas import tpu as pltpu
from jax.sharding import PartitionSpec as P


HEADS = 8
HEAD_DIM = 64
REACH = 2
WIDTHS = 2 * REACH + 1
PAIR = 2 * HEAD_DIM
ROWS = 8
TOTAL = HEAD_DIM
SHIFT = HEAD_DIM + ROWS
DEPTH = HEAD_DIM + 2 * ROWS
BLOCKED = -1e30
LOG2E = 1.4426950408889634
LIMIT = 2.0**80
F32 = jnp.float32
BF16 = jnp.bfloat16


def moved(value, axis, target):
    count = lax.axis_size(axis)
    pairs = [(source, target(source) % count) for source in range(count)]
    return lax.ppermute(value, axis, pairs)


def normalised(rows, gain):
    rows = rows.astype(F32)
    scale = lax.rsqrt(jnp.mean(rows * rows, axis=-1, keepdims=True) + 1e-06)
    return (rows * scale * gain).astype(BF16)


def fill_keys(normed, w_key, keys_ref):
    keys = jnp.dot(normed, w_key, preferred_element_type=F32).astype(BF16)
    for pair in range(HEADS // 2):
        keys_ref[pair] = keys[:, pair * PAIR : (pair + 1) * PAIR]


def fill_values(normed, w_value, values_ref):
    values = jnp.dot(normed, w_value, preferred_element_type=F32).astype(BF16)
    values_t = jnp.transpose(values)
    row = lax.broadcasted_iota(jnp.int32, (2 * ROWS, values_t.shape[1]), 0)
    ones = jnp.where(row < ROWS, 1.0, 0.0).astype(BF16)
    for head in range(HEADS):
        values_ref[head, :HEAD_DIM, :] = values_t[head * HEAD_DIM : (head + 1) * HEAD_DIM]
        values_ref[head, HEAD_DIM:, :] = ones


def bias_of(mask, own):
    tile = mask.shape[0]
    allowed = mask > 0
    if own:
        rows = lax.broadcasted_iota(jnp.int32, (tile, tile), 0)
        cols = lax.broadcasted_iota(jnp.int32, (tile, tile), 1)
        allowed = allowed | (rows == cols)
    bias = jnp.where(allowed, 0.0, BLOCKED).astype(BF16)
    return jnp.transpose(bias).astype(F32)


def attend(rows, gain, w_key, w_value, query_ref, bias_ref, keep, work, old, new):
    keys_ref, values_ref = work
    slot, first = keep
    count, tile = rows.shape[0], bias_ref.shape[-1]
    ahead = 1 if 2 * count > tile else 2
    normed = normalised(rows, gain)
    fill_keys(normed, w_key, keys_ref)

    def raw(head):
        return jnp.dot(keys_ref[head // 2], query_ref[head], preferred_element_type=F32)

    def scores(product):
        return product * LOG2E + bias_ref[slot, first : first + count]

    def mix(head, weight):
        return jnp.dot(values_ref[head], weight.astype(BF16), preferred_element_type=F32)

    pending = [raw(head) for head in range(ahead)]
    fill_values(normed, w_value, values_ref)
    strayed = jnp.zeros((ROWS, tile), F32)
    for head in range(HEADS):
        if head + ahead < HEADS:
            pending.append(raw(head + ahead))
        mixed = mix(head, jnp.exp2(scores(pending.pop(0))))
        if old is not None:
            mixed = old[head] + mixed
        new[head] = mixed
        total, shift = mixed[TOTAL:SHIFT], mixed[SHIFT:]
        fits = (total <= LIMIT) & (total >= 1.0 / LIMIT) & (shift == 0.0)
        strayed = jnp.where(fits, strayed, 1.0)

    @pl.when(jnp.max(strayed) > 0.0)
    def _():
        def one_head(head, carry):
            score = scores(raw(head))
            top = jnp.max(score, axis=0, keepdims=True)
            if old is not None:
                before = old[head, SHIFT : SHIFT + 1]
                top = jnp.maximum(before, top)
            mixed = mix(head, jnp.exp2(score - top))
            if old is not None:
                mixed = old[head] * jnp.exp2(before - top) + mixed
            new[head] = mixed
            new[head, SHIFT:] = jnp.broadcast_to(top, (ROWS, tile))
            return carry

        lax.fori_loop(0, HEADS, one_head, 0)


def first_kernel(
    which_ref, own_hbm, mask_hbm, gain_ref, w_query_hbm, w_key_hbm, w_value_hbm,
    query_ref, bias_ref, sum_ref,
    own_ref, mask_ref, w_query_ref, w_key_ref, w_value_ref,
    keys_ref, values_ref, sems,
):
    fetches = [
        pltpu.make_async_copy(source, target, sems.at[index])
        for index, (source, target) in enumerate(
            [
                (own_hbm, own_ref),
                (w_query_hbm, w_query_ref),
                (w_key_hbm, w_key_ref),
                (w_value_hbm, w_value_ref),
            ]
            + [(mask_hbm.at[0, offset], mask_ref.at[offset]) for offset in range(WIDTHS)]
        )
    ]
    for fetch in fetches:
        fetch.start()
    fetches[0].wait()
    normed = normalised(own_ref[...], gain_ref[...])
    fetches[1].wait()
    query = jnp.dot(normed, w_query_ref[...], preferred_element_type=F32).astype(BF16)
    query_t = jnp.transpose(query * jnp.asarray(HEAD_DIM ** (-0.5), BF16))
    tile = query_t.shape[1]
    for head in range(HEADS):
        half = (head % 2) * HEAD_DIM
        query_ref[head, half : half + HEAD_DIM, :] = query_t[
            head * HEAD_DIM : (head + 1) * HEAD_DIM
        ]
        query_ref[head, HEAD_DIM - half : PAIR - half, :] = jnp.zeros((HEAD_DIM, tile), BF16)
    for fetch in fetches[2:]:
        fetch.wait()
    for slot in range(WIDTHS):
        bias_ref[slot] = bias_of(mask_ref[which_ref[slot]], slot == 0)
    attend(
        own_ref[...], gain_ref[...], w_key_ref[...], w_value_ref[...], query_ref, bias_ref,
        (0, 0), (keys_ref, values_ref), None, sum_ref,
    )


def next_kernel(
    rows_ref, gain_ref, w_key_ref, w_value_ref, query_ref, bias_ref, sum_in,
    sum_ref, keys_ref, values_ref, *, slot, first=0,
):
    attend(
        rows_ref[...], gain_ref[...], w_key_ref[...], w_value_ref[...], query_ref, bias_ref,
        (slot, first), (keys_ref, values_ref), sum_in, sum_ref,
    )


def last_kernel(
    rows_ref, gain_ref, w_key_ref, w_value_ref, query_ref, bias_ref, sum_in,
    own_ref, w_out_ref, after_ref, stats_ref,
    keys_ref, values_ref, sum_ref, *, slot, first,
):
    next_kernel(
        rows_ref, gain_ref, w_key_ref, w_value_ref, query_ref, bias_ref, sum_in,
        sum_ref, keys_ref, values_ref, slot=slot, first=first,
    )
    mixed_t = jnp.concatenate(
        [
            (sum_ref[head, :HEAD_DIM] * (1.0 / sum_ref[head, TOTAL : TOTAL + 1])).astype(BF16)
            for head in range(HEADS)
        ],
        axis=0,
    )
    mixed = jnp.transpose(mixed_t)
    after = own_ref[...].astype(F32) + jnp.dot(
        mixed, w_out_ref[...], preferred_element_type=F32
    )
    after_ref[...] = after
    mean = jnp.mean(after, axis=0, keepdims=True)
    centered = after - mean
    stats_ref[0:1, :] = mean
    stats_ref[1:2, :] = jnp.sum(centered * centered, axis=0, keepdims=True)


def pick_kernel(flag_ref, yes_ref, no_ref, out_ref):
    first = yes_ref.shape[0] - out_ref.shape[0]
    for value, source in ((1, yes_ref), (0, no_ref)):

        @pl.when(flag_ref[WIDTHS] == value)
        def _():
            out_ref[...] = source[first:, :]


def joined(parts, rows):
    mean = sum(part[0] for part in parts) * (1.0 / len(parts))
    spread = sum(part[1] + rows * jnp.square(part[0] - mean) for part in parts)
    return jnp.stack([mean, spread])


def merged(stats, rows, axis):
    count = lax.axis_size(axis)
    step = 1
    while step < count:
        if count % (16 * step) == 0 and step == 1:
            stats = joined([stats, moved(stats, axis, lambda s: s ^ 1)], rows)
            side = lax.axis_index(axis) % 2
            last = moved(stats, axis, lambda s: s ^ 8)
            found = [
                moved(stats, axis, lambda s, peer=peer: s ^ (8 * (s % 2) + 2 * peer))
                for peer in (1, 2, 3)
            ]
            stats = joined([jnp.where(side == 0, stats, last)] + found, 2 * rows)
            stats = joined([stats, moved(stats, axis, lambda s: s ^ 1)], 8 * rows)
            step, rows = 16, 16 * rows
        else:
            stats = joined([stats, moved(stats, axis, lambda s: s ^ step)], rows)
            step, rows = 2 * step, 2 * rows
    return stats[0], stats[1] / rows


def body(
    atoms, edge_mask, norm_gain, w_query, w_key, w_value, w_out, bn_gain, bn_shift, w_up, w_down
):
    tile, width = atoms.shape
    place = lax.axis_index("blk") % 4
    sign = 1 - 2 * (place % 2)
    inner = (place + 1) // 2 % 2
    which = jnp.stack(
        [REACH + 0 * sign, REACH + sign, REACH - sign, REACH + 2 * sign, REACH - 2 * sign, inner]
    )
    across = moved(atoms, "blk", lambda s: s + 1 if s % 2 else s - 1)
    mate = moved(atoms, "blk", lambda s: s ^ 1)
    gain = norm_gain.reshape(1, width)

    vmem = pl.BlockSpec(memory_space=pltpu.VMEM)
    hbm = pl.BlockSpec(memory_space=pltpu.HBM)
    smem = pl.BlockSpec(memory_space=pltpu.SMEM)
    state = jax.ShapeDtypeStruct((HEADS, DEPTH, tile), F32)

    def work(rows):
        return [
            pltpu.VMEM((HEADS // 2, rows, PAIR), BF16),
            pltpu.VMEM((HEADS, DEPTH, rows), BF16),
        ]


    def params(mib):
        return pltpu.CompilerParams(vmem_limit_bytes=mib * 1024 * 1024)

    cost = pl.CostEstimate(
        flops=8 * tile * tile * width, bytes_accessed=4 * tile * width, transcendentals=0
    )

    passed = moved(across, "blk", lambda s: s ^ 1)
    half = tile // 2
    far0 = moved(atoms[:half], "blk", lambda s: s - 2 if s % 2 else s + 2)
    forward = pl.pallas_call(
        pick_kernel,
        in_specs=[smem, vmem, vmem],
        out_specs=vmem,
        out_shape=jax.ShapeDtypeStruct((half, width), BF16),
        compiler_params=params(2),
        name="pick_far",
    )(which, across, atoms)
    far1 = moved(forward, "blk", lambda s: s + (2, 3, -3, -2)[s % 4])

    query_heads, bias, sums = pl.pallas_call(
        first_kernel,
        in_specs=[smem, hbm, hbm, vmem, hbm, hbm, hbm],
        out_specs=[vmem] * 3,
        out_shape=[
            jax.ShapeDtypeStruct((HEADS, PAIR, tile), BF16),
            jax.ShapeDtypeStruct((WIDTHS, tile, tile), F32),
            state,
        ],
        scratch_shapes=[
            pltpu.VMEM((tile, width), BF16),
            pltpu.VMEM((WIDTHS, tile, tile), jnp.int32),
            pltpu.VMEM((width, width), BF16),
            pltpu.VMEM((width, width), BF16),
            pltpu.VMEM((width, width), BF16),
        ]
        + work(tile)
        + [pltpu.SemaphoreType.DMA((4 + WIDTHS,))],
        compiler_params=params(18),
        cost_estimate=cost,
        name="attend_own",
    )(which, *(pltpu.with_memory_space_constraint(value, pltpu.HBM) for value in (atoms, edge_mask)), gain,
      *(pltpu.with_memory_space_constraint(value, pltpu.HBM) for value in (w_query, w_key, w_value)))
    for rows, slot in ((mate, 1), (across, 2), (passed, 3), (far0, 4)):
        sums = pl.pallas_call(
            functools.partial(next_kernel, slot=slot),
            in_specs=[vmem] * 7,
            out_specs=vmem,
            out_shape=state,
            scratch_shapes=work(rows.shape[0]),
            compiler_params=params(12),
            cost_estimate=cost,
        )(rows, gain, w_key, w_value, query_heads, bias, sums)
    after, stats = pl.pallas_call(
        functools.partial(last_kernel, slot=WIDTHS - 1, first=half),
        in_specs=[vmem] * 9,
        out_specs=[vmem] * 2,
        out_shape=[
            jax.ShapeDtypeStruct((tile, width), F32),
            jax.ShapeDtypeStruct((2, width), F32),
        ],
        scratch_shapes=work(half) + [pltpu.VMEM(state.shape, F32)],
        compiler_params=params(12),
        cost_estimate=cost,
        name="attend_far1",
    )(far1, gain, w_key, w_value, query_heads, bias, sums, atoms, w_out)
    mean, var = merged(stats, tile, "blk")
    batched = ((after - mean) * lax.rsqrt(var + 1e-05) * bn_gain + bn_shift).astype(BF16)
    hidden = jax.nn.gelu(
        jnp.dot(batched, w_up, preferred_element_type=F32), approximate=True
    ).astype(BF16)
    return (after + jnp.dot(hidden, w_down, preferred_element_type=F32)).astype(BF16)


def solution(mesh):
    rows = P(("grp", "blk"), None)
    placed = (rows, P(("grp", "blk"), None, None, None)) + (P(),) * 9


    return jax.shard_map(body, mesh=mesh, in_specs=placed, out_specs=rows, check_vma=False)
```

profile of v0, /device:TPU:0, one launch (start us, length us, event | category | flops | bytes accessed | tf_op | source)
XLA Modules:
  0.0 82.7 jit_solution(14551032227255156088)
XLA Ops:
  0.0 0.0 copy-start
  0.0 5.5 %collective-permute-start = (bf16[512,512]{1,0:T(8,128)(2,1)}, bf16[512,512]{1,0:T(8,128)(2,1)S(1)}, u32[]{:S(2)}, u32[]{:S(2)}) collective-permute-start(bf16[512,512]{1,0:T(8,128)(2,1)} %own_ref.1), channel_id=1, source_target_pairs={{0,15},{1,2},{2,1},{3,4},{4,3},{5,6},{6,5},{7,8},{8,7},{9,10},{10,... | collective-permute-start | bytes 1572872 | tf_op jit(solution)/shard_map/ppermute | solution.py:30
  5.5 0.0 collective-permute-start.4
  5.5 7.2 %collective-permute-done.yes_ref.rows_ref = bf16[512,512]{1,0:T(8,128)(2,1)S(1)} collective-permute-done((bf16[512,512]{1,0:T(8,128)(2,1)}, bf16[512,512]{1,0:T(8,128)(2,1)S(1)}, u32[]{:S(2)}, u32[]{:S(2)}) %collective-permute-start) | collective-permute-done | bytes 524320 | tf_op jit(solution)/shard_map/ppermute | solution.py:30
  12.6 3.2 %collective-permute-start.3 = (bf16[512,512]{1,0:T(8,128)(2,1)S(1)}, bf16[512,512]{1,0:T(8,128)(2,1)S(1)}, u32[]{:S(2)}, u32[]{:S(2)}) collective-permute-start(bf16[512,512]{1,0:T(8,128)(2,1)S(1)} %collective-permute-done.yes_ref.rows_ref), channel_id=1, source_target_pairs={{0,1},{1,0},{2,3},{3,2},{4,5},{5,4},{6,7},{7,6},{8,9},{9,8},{10,11... | collective-permute-start | bytes 1572872 | tf_op jit(solution)/shard_map/ppermute | solution.py:30
  15.8 1.0 %slice.52 = bf16[256,512]{1,0:T(8,128)(2,1)S(1)} slice(bf16[512,512]{1,0:T(8,128)(2,1)} %own_ref.1), slice={[0:256], [0:512]} | slice | bytes 524288 | tf_op jit(solution)/shard_map/slice | solution.py:265
  16.8 1.7 %collective-permute-start.2 = (bf16[256,512]{1,0:T(8,128)(2,1)S(1)}, bf16[256,512]{1,0:T(8,128)(2,1)S(1)}, u32[]{:S(2)}, u32[]{:S(2)}) collective-permute-start(bf16[256,512]{1,0:T(8,128)(2,1)S(1)} %slice.52), channel_id=1, source_target_pairs={{0,2},{1,15},{2,4},{3,1},{4,6},{5,3},{6,8},{7,5},{8,10},{9,7},{10,... | collective-permute-start | bytes 786440 | tf_op jit(solution)/shard_map/ppermute | solution.py:30
  18.5 0.1 stack.34.flag_ref.which_ref
  18.5 0.0 copy-start.5
  18.5 0.7 copy-done.5
  19.2 0.0 copy-start.3
  19.2 11.9 %attend_own.1 = (bf16[8,128,512]{2,1,0:T(8,128)(2,1)S(1)}, f32[5,512,512]{2,1,0:T(8,128)S(1)}, f32[8,80,512]{2,1,0:T(8,128)S(1)}) custom-call(s32[6]{0:T(128)S(1)} %stack.34.flag_ref.which_ref, bf16[512,512]{1,0:T(8,128)(2,1)} %own_ref.1, s32[1,5,512,512]{3,2,1,0:T(8,128)} %mask_hbm.1, f32[1,512]{1,0:T(1,128)S(1)} %bitcast.10, bf16[512,512]{1,0:T(8,128)(2,1)} %w_query_hbm.1, ...), custom_call_target="tpu_custom_call" | custom-call | flops 1073741824 | bytes 1048576 | tf_op jit(solution)/shard_map/attend_own/pallas_call | solution.py:276
  31.2 0.0 copy-done.3
  31.2 0.6 pick_far.1
  31.8 1.5 %collective-permute-start.1 = (bf16[256,512]{1,0:T(8,128)(2,1)S(1)}, bf16[256,512]{1,0:T(8,128)(2,1)S(1)}, u32[]{:S(2)}, u32[]{:S(2)}) collective-permute-start(bf16[256,512]{1,0:T(8,128)(2,1)S(1)} %pick_far.1), channel_id=1, source_target_pairs={{0,2},{1,4},{2,15},{3,1},{4,6},{5,8},{6,3},{7,5},{8,10},{9,12},{10... | collective-permute-start | bytes 786440 | tf_op jit(solution)/shard_map/ppermute | solution.py:30
  33.2 0.0 collective-permute-done.4.rows_ref
  33.2 0.0 copy-done.1
  33.2 0.0 copy-done.2
  33.2 7.5 %shard_map.109.sum_in = f32[8,80,512]{2,1,0:T(8,128)S(1)} custom-call(bf16[512,512]{1,0:T(8,128)(2,1)S(1)} %collective-permute-done.4.rows_ref, f32[1,512]{1,0:T(1,128)S(1)} %bitcast.11, bf16[512,512]{1,0:T(8,128)(2,1)S(1)} %copy-done.1, bf16[512,512]{1,0:T(8,128)(2,1)S(1)} %copy-done.2, bf16[8,128,512]{2,1,0:T(8,128)(2,1)S(1)} %get-tuple-element.10.query_ref, ...), custom_call_target="tpu_custom_call" | custom-call | flops 1073741824 | bytes 1048576 | tf_op jit(solution)/shard_map/pallas_call | solution.py:300
  40.8 7.7 %shard_map.110.sum_in = f32[8,80,512]{2,1,0:T(8,128)S(1)} custom-call(bf16[512,512]{1,0:T(8,128)(2,1)S(1)} %collective-permute-done.yes_ref.rows_ref, f32[1,512]{1,0:T(1,128)S(1)} %bitcast.12, bf16[512,512]{1,0:T(8,128)(2,1)S(1)} %copy-done.1, bf16[512,512]{1,0:T(8,128)(2,1)S(1)} %copy-done.2, bf16[8,128,512]{2,1,0:T(8,128)(2,1)S(1)} %get-tuple-element.10.query_ref, ...), custom_call_target="tpu_custom_call" | custom-call | flops 1073741824 | bytes 1048576 | tf_op jit(solution)/shard_map/pallas_call | solution.py:300
  48.5 0.0 collective-permute-done.3.rows_ref
  48.5 7.6 %shard_map.111.sum_in = f32[8,80,512]{2,1,0:T(8,128)S(1)} custom-call(bf16[512,512]{1,0:T(8,128)(2,1)S(1)} %collective-permute-done.3.rows_ref, f32[1,512]{1,0:T(1,128)S(1)} %bitcast.13, bf16[512,512]{1,0:T(8,128)(2,1)S(1)} %copy-done.1, bf16[512,512]{1,0:T(8,128)(2,1)S(1)} %copy-done.2, bf16[8,128,512]{2,1,0:T(8,128)(2,1)S(1)} %get-tuple-element.10.query_ref, ...), custom_call_target="tpu_custom_call" | custom-call | flops 1073741824 | bytes 1048576 | tf_op jit(solution)/shard_map/pallas_call | solution.py:300
  56.1 0.0 copy-start.4
  56.1 0.0 collective-permute-done.2.rows_ref
  56.1 5.3 %shard_map.112.sum_in = f32[8,80,512]{2,1,0:T(8,128)S(1)} custom-call(bf16[256,512]{1,0:T(8,128)(2,1)S(1)} %collective-permute-done.2.rows_ref, f32[1,512]{1,0:T(1,128)S(1)} %bitcast.14, bf16[512,512]{1,0:T(8,128)(2,1)S(1)} %copy-done.1, bf16[512,512]{1,0:T(8,128)(2,1)S(1)} %copy-done.2, bf16[8,128,512]{2,1,0:T(8,128)(2,1)S(1)} %get-tuple-element.10.query_ref, ...), custom_call_target="tpu_custom_call" | custom-call | flops 1073741824 | bytes 1048576 | tf_op jit(solution)/shard_map/pallas_call | solution.py:300
  61.4 0.0 copy-start.6
  61.4 0.0 copy-start.7
  61.5 0.0 copy-start.8
  61.5 0.0 collective-permute-done.1.rows_ref
  61.5 0.0 copy-done.4
  61.5 5.9 %attend_far1.1 = (f32[512,512]{1,0:T(8,128)S(1)}, f32[2,512]{1,0:T(2,128)S(1)}) custom-call(bf16[256,512]{1,0:T(8,128)(2,1)S(1)} %collective-permute-done.1.rows_ref, f32[1,512]{1,0:T(1,128)S(1)} %bitcast.15, bf16[512,512]{1,0:T(8,128)(2,1)S(1)} %copy-done.1, bf16[512,512]{1,0:T(8,128)(2,1)S(1)} %copy-done.2, ...), custom_call_target="tpu_custom_call" | custom-call | flops 1073741824 | bytes 1048576 | tf_op jit(solution)/shard_map/attend_far1/pallas_call | solution.py:309
  67.4 2.0 %collective-permute-start.5 = (f32[2,512]{1,0:T(2,128)S(1)}, f32[2,512]{1,0:T(2,128)S(1)}, u32[]{:S(2)}, u32[]{:S(2)}) collective-permute-start(f32[2,512]{1,0:T(2,128)S(1)} %get-tuple-element.14), channel_id=1, source_target_pairs={{0,1},{1,0},{2,3},{3,2},{4,5},{5,4},{6,7},{7,6},{8,9},{9,8},{10,11... | collective-permute-start | bytes 12296 | tf_op jit(solution)/shard_map/ppermute | solution.py:30
  69.4 0.8 collective-permute-done.5
  70.2 1.1 %collective-permute-start.6 = (f32[2,512]{1,0:T(2,128)S(1)}, f32[2,512]{1,0:T(2,128)S(1)}, u32[]{:S(2)}, u32[]{:S(2)}) collective-permute-start(f32[2,512]{1,0:T(2,128)S(1)} %pad_maximum_fusion), channel_id=1, source_target_pairs={{0,8},{1,9},{2,10},{3,11},{4,12},{5,13},{6,14},{7,15},{8,0},{9,1},... | collective-permute-start | bytes 12296 | tf_op jit(solution)/shard_map/ppermute | solution.py:30
  71.3 0.7 collective-permute-start.7
  72.1 0.9 %collective-permute-start.8 = (f32[2,512]{1,0:T(2,128)S(1)}, f32[2,512]{1,0:T(2,128)S(1)}, u32[]{:S(2)}, u32[]{:S(2)}) collective-permute-start(f32[2,512]{1,0:T(2,128)S(1)} %pad_maximum_fusion), channel_id=1, source_target_pairs={{0,4},{1,13},{2,6},{3,15},{4,0},{5,9},{6,2},{7,11},{8,12},{9,5},{1... | collective-permute-start | bytes 12296 | tf_op jit(solution)/shard_map/ppermute | solution.py:30
  73.0 1.8 %collective-permute-start.9 = (f32[2,512]{1,0:T(2,128)S(1)}, f32[2,512]{1,0:T(2,128)S(1)}, u32[]{:S(2)}, u32[]{:S(2)}) collective-permute-start(f32[2,512]{1,0:T(2,128)S(1)} %pad_maximum_fusion), channel_id=1, source_target_pairs={{0,6},{1,15},{2,4},{3,13},{4,2},{5,11},{6,0},{7,9},{8,14},{9,7},{1... | collective-permute-start | bytes 12296 | tf_op jit(solution)/shard_map/ppermute | solution.py:30
  74.8 0.0 collective-permute-done.6
  74.8 0.1 collective-permute-done.7
  74.9 0.7 collective-permute-done.8
  75.7 1.8 %collective-permute-done.9 = f32[2,512]{1,0:T(2,128)S(1)} collective-permute-done((f32[2,512]{1,0:T(2,128)S(1)}, f32[2,512]{1,0:T(2,128)S(1)}, u32[]{:S(2)}, u32[]{:S(2)}) %collective-permute-start.9) | collective-permute-done | bytes 4128 | tf_op jit(solution)/shard_map/ppermute | solution.py:30
  77.6 2.0 %collective-permute-start.10 = (f32[2,512]{1,0:T(2,128)S(1)}, f32[2,512]{1,0:T(2,128)S(1)}, u32[]{:S(2)}, u32[]{:S(2)}) collective-permute-start(f32[2,512]{1,0:T(2,128)S(1)} %pad_maximum_fusion.1), channel_id=1, source_target_pairs={{0,1},{1,0},{2,3},{3,2},{4,5},{5,4},{6,7},{7,6},{8,9},{9,8},{10,11... | collective-permute-start | bytes 12296 | tf_op jit(solution)/shard_map/ppermute | solution.py:30
  79.6 0.8 collective-permute-done.10
  80.4 0.0 copy-done
  80.4 0.0 copy-done.6
  80.5 0.0 copy-done.7
  80.5 0.0 copy-done.8
  80.5 2.2 %fusion.8 = bf16[512,512]{1,0:T(8,128)(2,1)} fusion(f32[512,512]{1,0:T(8,128)S(1)} %get-tuple-element.13, bf16[1024,512]{1,0:T(8,128)(2,1)S(1)} %copy-done, bf16[512,1024]{1,0:T(8,128)(2,1)S(1)} %copy-done.6, f32[512]{0:T(512)S(1)} %copy-done.7, f32[512]{0:T(512)S(1)} %copy-done.8, f32[512]{0:T(512)S(1)} %bitcast.17, f32[512]{0:T(512)S(1)} %bitcast.16), kind=kOutput, calls=%fused_computation.10 | convolution fusion | flops 1080295424 | bytes 3678208 | tf_op jit(solution)/shard_map/dot_general | solution.py:327
  (8 shorter events, 0.1 us)
Async XLA Ops:
  0.0 80.4 %copy-start = (bf16[1024,512]{1,0:T(8,128)(2,1)S(1)}, bf16[1024,512]{1,0:T(8,128)(2,1)}, u32[]{:S(2)}) copy-start(bf16[1024,512]{1,0:T(8,128)(2,1)} %param.21) | copy-start | bytes 3145732
  0.0 12.6 %collective-permute-start = (bf16[512,512]{1,0:T(8,128)(2,1)}, bf16[512,512]{1,0:T(8,128)(2,1)S(1)}, u32[]{:S(2)}, u32[]{:S(2)}) collective-permute-start(bf16[512,512]{1,0:T(8,128)(2,1)} %own_ref.1), channel_id=1, source_target_pairs={{0,15},{1,2},{2,1},{3,4},{4,3},{5,6},{6,5},{7,8},{8,7},{9,10},{10,... | collective-permute-start | bytes 1572872 | tf_op jit(solution)/shard_map/ppermute | solution.py:30
  5.5 27.8 %collective-permute-start.4 = (bf16[512,512]{1,0:T(8,128)(2,1)}, bf16[512,512]{1,0:T(8,128)(2,1)S(1)}, u32[]{:S(2)}, u32[]{:S(2)}) collective-permute-start(bf16[512,512]{1,0:T(8,128)(2,1)} %own_ref.1), channel_id=1, source_target_pairs={{0,1},{1,0},{2,3},{3,2},{4,5},{5,4},{6,7},{7,6},{8,9},{9,8},{10,11... | collective-permute-start | bytes 1572872 | tf_op jit(solution)/shard_map/ppermute | solution.py:30
  12.6 35.9 %collective-permute-start.3 = (bf16[512,512]{1,0:T(8,128)(2,1)S(1)}, bf16[512,512]{1,0:T(8,128)(2,1)S(1)}, u32[]{:S(2)}, u32[]{:S(2)}) collective-permute-start(bf16[512,512]{1,0:T(8,128)(2,1)S(1)} %collective-permute-done.yes_ref.rows_ref), channel_id=1, source_target_pairs={{0,1},{1,0},{2,3},{3,2},{4,5},{5,4},{6,7},{7,6},{8,9},{9,8},{10,11... | collective-permute-start | bytes 1572872 | tf_op jit(solution)/shard_map/ppermute | solution.py:30
  16.8 39.3 %collective-permute-start.2 = (bf16[256,512]{1,0:T(8,128)(2,1)S(1)}, bf16[256,512]{1,0:T(8,128)(2,1)S(1)}, u32[]{:S(2)}, u32[]{:S(2)}) collective-permute-start(bf16[256,512]{1,0:T(8,128)(2,1)S(1)} %slice.52), channel_id=1, source_target_pairs={{0,2},{1,15},{2,4},{3,1},{4,6},{5,3},{6,8},{7,5},{8,10},{9,7},{10,... | collective-permute-start | bytes 786440 | tf_op jit(solution)/shard_map/ppermute | solution.py:30
  18.5 0.7 copy-start.5
  19.2 12.0 %copy-start.3 = (bf16[512,512]{1,0:T(8,128)(2,1)S(1)}, bf16[512,512]{1,0:T(8,128)(2,1)}, u32[]{:S(2)}) copy-start(bf16[512,512]{1,0:T(8,128)(2,1)} %own_ref.1) | copy-start | bytes 1572868
  19.2 14.0 %copy-start.1 = (bf16[512,512]{1,0:T(8,128)(2,1)S(1)}, bf16[512,512]{1,0:T(8,128)(2,1)}, u32[]{:S(2)}) copy-start(bf16[512,512]{1,0:T(8,128)(2,1)} %w_key_ref.9) | copy-start | bytes 1572868
  19.2 14.0 %copy-start.2 = (bf16[512,512]{1,0:T(8,128)(2,1)S(1)}, bf16[512,512]{1,0:T(8,128)(2,1)}, u32[]{:S(2)}) copy-start(bf16[512,512]{1,0:T(8,128)(2,1)} %w_value_ref.9) | copy-start | bytes 1572868
  31.8 29.7 %collective-permute-start.1 = (bf16[256,512]{1,0:T(8,128)(2,1)S(1)}, bf16[256,512]{1,0:T(8,128)(2,1)S(1)}, u32[]{:S(2)}, u32[]{:S(2)}) collective-permute-start(bf16[256,512]{1,0:T(8,128)(2,1)S(1)} %pick_far.1), channel_id=1, source_target_pairs={{0,2},{1,4},{2,15},{3,1},{4,6},{5,8},{6,3},{7,5},{8,10},{9,12},{10... | collective-permute-start | bytes 786440 | tf_op jit(solution)/shard_map/ppermute | solution.py:30
  56.1 5.4 %copy-start.4 = (bf16[512,512]{1,0:T(8,128)(2,1)S(1)}, bf16[512,512]{1,0:T(8,128)(2,1)}, u32[]{:S(2)}) copy-start(bf16[512,512]{1,0:T(8,128)(2,1)} %w_out_ref.1) | copy-start | bytes 1572868
  61.4 19.0 %copy-start.6 = (bf16[512,1024]{1,0:T(8,128)(2,1)S(1)}, bf16[512,1024]{1,0:T(8,128)(2,1)}, u32[]{:S(2)}) copy-start(bf16[512,1024]{1,0:T(8,128)(2,1)} %param.20) | copy-start | bytes 3145732
  61.4 19.0 %copy-start.7 = (f32[512]{0:T(512)S(1)}, f32[512]{0:T(512)}, u32[]{:S(2)}) copy-start(f32[512]{0:T(512)} %param.19) | copy-start | bytes 6148
  61.5 19.0 %copy-start.8 = (f32[512]{0:T(512)S(1)}, f32[512]{0:T(512)}, u32[]{:S(2)}) copy-start(f32[512]{0:T(512)} %param.18) | copy-start | bytes 6148
  67.4 2.8 %collective-permute-start.5 = (f32[2,512]{1,0:T(2,128)S(1)}, f32[2,512]{1,0:T(2,128)S(1)}, u32[]{:S(2)}, u32[]{:S(2)}) collective-permute-start(f32[2,512]{1,0:T(2,128)S(1)} %get-tuple-element.14), channel_id=1, source_target_pairs={{0,1},{1,0},{2,3},{3,2},{4,5},{5,4},{6,7},{7,6},{8,9},{9,8},{10,11... | collective-permute-start | bytes 12296 | tf_op jit(solution)/shard_map/ppermute | solution.py:30
  70.2 4.6 %collective-permute-start.6 = (f32[2,512]{1,0:T(2,128)S(1)}, f32[2,512]{1,0:T(2,128)S(1)}, u32[]{:S(2)}, u32[]{:S(2)}) collective-permute-start(f32[2,512]{1,0:T(2,128)S(1)} %pad_maximum_fusion), channel_id=1, source_target_pairs={{0,8},{1,9},{2,10},{3,11},{4,12},{5,13},{6,14},{7,15},{8,0},{9,1},... | collective-permute-start | bytes 12296 | tf_op jit(solution)/shard_map/ppermute | solution.py:30
  71.3 3.6 %collective-permute-start.7 = (f32[2,512]{1,0:T(2,128)S(1)}, f32[2,512]{1,0:T(2,128)S(1)}, u32[]{:S(2)}, u32[]{:S(2)}) collective-permute-start(f32[2,512]{1,0:T(2,128)S(1)} %pad_maximum_fusion), channel_id=1, source_target_pairs={{0,2},{1,11},{2,0},{3,9},{4,6},{5,15},{6,4},{7,13},{8,10},{9,3},{1... | collective-permute-start | bytes 12296 | tf_op jit(solution)/shard_map/ppermute | solution.py:30
  72.1 3.6 %collective-permute-start.8 = (f32[2,512]{1,0:T(2,128)S(1)}, f32[2,512]{1,0:T(2,128)S(1)}, u32[]{:S(2)}, u32[]{:S(2)}) collective-permute-start(f32[2,512]{1,0:T(2,128)S(1)} %pad_maximum_fusion), channel_id=1, source_target_pairs={{0,4},{1,13},{2,6},{3,15},{4,0},{5,9},{6,2},{7,11},{8,12},{9,5},{1... | collective-permute-start | bytes 12296 | tf_op jit(solution)/shard_map/ppermute | solution.py:30
  73.0 4.5 %collective-permute-start.9 = (f32[2,512]{1,0:T(2,128)S(1)}, f32[2,512]{1,0:T(2,128)S(1)}, u32[]{:S(2)}, u32[]{:S(2)}) collective-permute-start(f32[2,512]{1,0:T(2,128)S(1)} %pad_maximum_fusion), channel_id=1, source_target_pairs={{0,6},{1,15},{2,4},{3,13},{4,2},{5,11},{6,0},{7,9},{8,14},{9,7},{1... | collective-permute-start | bytes 12296 | tf_op jit(solution)/shard_map/ppermute | solution.py:30
  77.6 2.8 %collective-permute-start.10 = (f32[2,512]{1,0:T(2,128)S(1)}, f32[2,512]{1,0:T(2,128)S(1)}, u32[]{:S(2)}, u32[]{:S(2)}) collective-permute-start(f32[2,512]{1,0:T(2,128)S(1)} %pad_maximum_fusion.1), channel_id=1, source_target_pairs={{0,1},{1,0},{2,3},{3,2},{4,5},{5,4},{6,7},{7,6},{8,9},{9,8},{10,11... | collective-permute-start | bytes 12296 | tf_op jit(solution)/shard_map/ppermute | solution.py:30
where the time goes:
time: 82.9 us; the launch traced here: 82.7 us
  Pallas kernels  46.6 us (56%)
  starting transfers between devices  20.4 us (25%)
  waiting for transfers between devices  11.5 us (14%)
  matrix products  2.25 us (3%)
  local copies, waits for them, and re-layouts  1.77 us (2%)
    pallas_call x4, Pallas kernels, body(): pl.pallas_call(functools.partial(next_kernel, slot=slot), in_specs=[vmem]...  28.1 us
    ppermute x11, starting transfers between devices, moved(): return lax.ppermute(value, axis, pairs)  20.4 us
    pallas_call x1, Pallas kernels, body(): pl.pallas_call(first_kernel, in_specs=[smem, hbm, hbm, vmem, hbm, hbm, hb...  11.9 us
    ppermute x11, waiting for transfers between devices, moved(): return lax.ppermute(value, axis, pairs)  11.5 us
    pallas_call x1, Pallas kernels, body(): pl.pallas_call(functools.partial(last_kernel, slot=WIDTHS - 1, first=half...  5.92 us
    dot_general x1, matrix products, body(): jnp.dot(hidden, w_down, preferred_element_type=F32)  2.25 us
  transfers between devices with their start and end apart: 11, of which 6 were waited for; matrix products, arithmetic and copies ran while one was open for 1% of the time, Pallas kernels for 49%

commit v1 on v0

--- a/solution.py
+++ b/solution.py
@@ -113,9 +113,9 @@
 
 
 def first_kernel(
-    which_ref, own_hbm, mask_hbm, gain_ref, w_query_hbm, w_key_hbm, w_value_hbm,
-    query_ref, bias_ref, sum_ref,
-    own_ref, mask_ref, w_query_ref, w_key_ref, w_value_ref,
+    which_ref, own_hbm, mask_hbm, gain_hbm, w_query_hbm, w_key_hbm, w_value_hbm,
+    query_ref, bias_ref, sum_ref, piece_ref,
+    own_ref, mask_ref, gain_ref, w_query_ref, w_key_ref, w_value_ref,
     keys_ref, values_ref, sems,
 ):
     fetches = [
@@ -123,6 +123,7 @@
         for index, (source, target) in enumerate(
             [
                 (own_hbm, own_ref),
+                (gain_hbm, gain_ref),
                 (w_query_hbm, w_query_ref),
                 (w_key_hbm, w_key_ref),
                 (w_value_hbm, w_value_ref),
@@ -133,8 +134,10 @@
     for fetch in fetches:
         fetch.start()
     fetches[0].wait()
+    piece_ref[...] = own_ref[: piece_ref.shape[0], :]
+    fetches[1].wait()
     normed = normalised(own_ref[...], gain_ref[...])
-    fetches[1].wait()
+    fetches[2].wait()
     query = jnp.dot(normed, w_query_ref[...], preferred_element_type=F32).astype(BF16)
     query_t = jnp.transpose(query * jnp.asarray(HEAD_DIM ** (-0.5), BF16))
     tile = query_t.shape[1]
@@ -144,7 +147,7 @@
             head * HEAD_DIM : (head + 1) * HEAD_DIM
         ]
         query_ref[head, HEAD_DIM - half : PAIR - half, :] = jnp.zeros((HEAD_DIM, tile), BF16)
-    for fetch in fetches[2:]:
+    for fetch in fetches[3:]:
         fetch.wait()
     for slot in range(WIDTHS):
         bias_ref[slot] = bias_of(mask_ref[which_ref[slot]], slot == 0)
@@ -262,7 +265,6 @@
 
     passed = moved(across, "blk", lambda s: s ^ 1)
     half = tile // 2
-    far0 = moved(atoms[:half], "blk", lambda s: s - 2 if s % 2 else s + 2)
     forward = pl.pallas_call(
         pick_kernel,
         in_specs=[smem, vmem, vmem],
@@ -273,29 +275,37 @@
     )(which, across, atoms)
     far1 = moved(forward, "blk", lambda s: s + (2, 3, -3, -2)[s % 4])
 
-    query_heads, bias, sums = pl.pallas_call(
+    query_heads, bias, sums, piece = pl.pallas_call(
         first_kernel,
-        in_specs=[smem, hbm, hbm, vmem, hbm, hbm, hbm],
-        out_specs=[vmem] * 3,
+        in_specs=[smem] + [hbm] * 6,
+        out_specs=[vmem] * 4,
         out_shape=[
             jax.ShapeDtypeStruct((HEADS, PAIR, tile), BF16),
             jax.ShapeDtypeStruct((WIDTHS, tile, tile), F32),
             state,
+            jax.ShapeDtypeStruct((half, width), BF16),
         ],
         scratch_shapes=[
             pltpu.VMEM((tile, width), BF16),
             pltpu.VMEM((WIDTHS, tile, tile), jnp.int32),
+            pltpu.VMEM((1, width), F32),
             pltpu.VMEM((width, width), BF16),
             pltpu.VMEM((width, width), BF16),
             pltpu.VMEM((width, width), BF16),
         ]
         + work(tile)
-        + [pltpu.SemaphoreType.DMA((4 + WIDTHS,))],
+        + [pltpu.SemaphoreType.DMA((5 + WIDTHS,))],
         compiler_params=params(18),
         cost_estimate=cost,
         name="attend_own",
-    )(which, *(pltpu.with_memory_space_constraint(value, pltpu.HBM) for value in (atoms, edge_mask)), gain,
-      *(pltpu.with_memory_space_constraint(value, pltpu.HBM) for value in (w_query, w_key, w_value)))
+    )(
+        which,
+        *(
+            pltpu.with_memory_space_constraint(value, pltpu.HBM)
+            for value in (atoms, edge_mask, gain, w_query, w_key, w_value)
+        ),
+    )
+    far0 = moved(piece, "blk", lambda s: s - 2 if s % 2 else s + 2)
     for rows, slot in ((mate, 1), (across, 2), (passed, 3), (far0, 4)):
         sums = pl.pallas_call(
             functools.partial(next_kernel, slot=slot),

time: 82.9 us -> 81.8 us (0.987)
  local copies, waits for them, and re-layouts: 1.77 us -> 0.13 us
    slice x1 -> x0, local copies, waits for them, and re-layouts: 0.97 us -> none  [body(): far0 = moved(atoms[:half], 'blk', lambda s: s - 2 if s % 2 else s + 2)]
  transfers between devices with their start and end apart: 11 -> 11, of which waited for: 6 -> 6; matrix products, arithmetic and copies ran while one was open for 1% -> 0% of each run, Pallas kernels for 49% -> 50%
where the time goes in v1:
time: 81.8 us; the launch traced here: 81.6 us
  Pallas kernels  47.1 us (58%)
  starting transfers between devices  20.3 us (25%)
  waiting for transfers between devices  11.5 us (14%)
  matrix products  2.24 us (3%)
    pallas_call x4, Pallas kernels, body(): pl.pallas_call(functools.partial(next_kernel, slot=slot), in_specs=[vmem]...  28.6 us
    ppermute x11, starting transfers between devices, moved(): return lax.ppermute(value, axis, pairs)  20.3 us
    pallas_call x1, Pallas kernels, body(): pl.pallas_call(first_kernel, in_specs=[smem] + [hbm] * 6, out_specs=[vmem...  12 us
    ppermute x11, waiting for transfers between devices, moved(): return lax.ppermute(value, axis, pairs)  11.5 us
    pallas_call x1, Pallas kernels, body(): pl.pallas_call(functools.partial(last_kernel, slot=WIDTHS - 1, first=half...  5.96 us
    dot_general x1, matrix products, body(): jnp.dot(hidden, w_down, preferred_element_type=F32)  2.24 us
  transfers between devices with their start and end apart: 11, of which 6 were waited for; matrix products, arithmetic and copies ran while one was open for 0% of the time, Pallas kernels for 50%

profile of v1, /device:TPU:0, one launch (start us, length us, event | category | flops | bytes accessed | tf_op | source)
XLA Modules:
  0.0 81.6 jit_solution(4691147032046560088)
XLA Ops:
  0.0 0.0 copy-start
  0.0 5.5 %collective-permute-start = (bf16[512,512]{1,0:T(8,128)(2,1)}, bf16[512,512]{1,0:T(8,128)(2,1)S(1)}, u32[]{:S(2)}, u32[]{:S(2)}) collective-permute-start(bf16[512,512]{1,0:T(8,128)(2,1)} %own_ref.1), channel_id=1, source_target_pairs={{0,15},{1,2},{2,1},{3,4},{4,3},{5,6},{6,5},{7,8},{8,7},{9,10},{10,... | collective-permute-start | bytes 1572872 | tf_op jit(solution)/shard_map/ppermute | solution.py:30
  5.5 0.0 collective-permute-start.4
  5.5 7.2 %collective-permute-done.yes_ref.rows_ref = bf16[512,512]{1,0:T(8,128)(2,1)S(1)} collective-permute-done((bf16[512,512]{1,0:T(8,128)(2,1)}, bf16[512,512]{1,0:T(8,128)(2,1)S(1)}, u32[]{:S(2)}, u32[]{:S(2)}) %collective-permute-start) | collective-permute-done | bytes 524320 | tf_op jit(solution)/shard_map/ppermute | solution.py:30
  12.6 3.2 %collective-permute-start.3 = (bf16[512,512]{1,0:T(8,128)(2,1)S(1)}, bf16[512,512]{1,0:T(8,128)(2,1)S(1)}, u32[]{:S(2)}, u32[]{:S(2)}) collective-permute-start(bf16[512,512]{1,0:T(8,128)(2,1)S(1)} %collective-permute-done.yes_ref.rows_ref), channel_id=1, source_target_pairs={{0,1},{1,0},{2,3},{3,2},{4,5},{5,4},{6,7},{7,6},{8,9},{9,8},{10,11... | collective-permute-start | bytes 1572872 | tf_op jit(solution)/shard_map/ppermute | solution.py:30
  15.8 0.1 stack.34.flag_ref.which_ref
  15.9 0.0 copy-start.3
  15.9 0.0 copy-start.1
  15.9 0.0 copy-start.5
  15.9 12.0 %attend_own.1 = (bf16[8,128,512]{2,1,0:T(8,128)(2,1)S(1)}, f32[5,512,512]{2,1,0:T(8,128)S(1)}, f32[8,80,512]{2,1,0:T(8,128)S(1)}, bf16[256,512]{1,0:T(8,128)(2,1)S(1)}) custom-call(s32[6]{0:T(128)S(1)} %stack.34.flag_ref.which_ref, bf16[512,512]{1,0:T(8,128)(2,1)} %own_ref.1, s32[1,5,512,512]{3,2,1,0:T(8,128)} %mask_hbm.1, f32[1,512]{1,0:T(1,128)} %bitcast.10, ...), custom_call_target="tpu_custom_call" | custom-call | flops 1073741824 | bytes 1048576 | tf_op jit(solution)/shard_map/attend_own/pallas_call | solution.py:278
  27.9 1.7 %collective-permute-start.2 = (bf16[256,512]{1,0:T(8,128)(2,1)S(1)}, bf16[256,512]{1,0:T(8,128)(2,1)S(1)}, u32[]{:S(2)}, u32[]{:S(2)}) collective-permute-start(bf16[256,512]{1,0:T(8,128)(2,1)S(1)} %get-tuple-element.13), channel_id=1, source_target_pairs={{0,2},{1,15},{2,4},{3,1},{4,6},{5,3},{6,8},{7,5},{8,10},{9,7},{10,... | collective-permute-start | bytes 786440 | tf_op jit(solution)/shard_map/ppermute | solution.py:30
  29.6 0.0 copy-done.3
  29.6 0.6 pick_far.1
  30.2 1.5 %collective-permute-start.1 = (bf16[256,512]{1,0:T(8,128)(2,1)S(1)}, bf16[256,512]{1,0:T(8,128)(2,1)S(1)}, u32[]{:S(2)}, u32[]{:S(2)}) collective-permute-start(bf16[256,512]{1,0:T(8,128)(2,1)S(1)} %pick_far.1), channel_id=1, source_target_pairs={{0,2},{1,4},{2,15},{3,1},{4,6},{5,8},{6,3},{7,5},{8,10},{9,12},{10... | collective-permute-start | bytes 786440 | tf_op jit(solution)/shard_map/ppermute | solution.py:30
  31.7 0.0 collective-permute-done.4.rows_ref
  31.7 0.0 copy-done.1
  31.7 0.0 copy-done.2
  31.7 0.0 copy-done.5
  31.7 7.7 %shard_map.109.sum_in = f32[8,80,512]{2,1,0:T(8,128)S(1)} custom-call(bf16[512,512]{1,0:T(8,128)(2,1)S(1)} %collective-permute-done.4.rows_ref, f32[1,512]{1,0:T(1,128)S(1)} %bitcast.11, bf16[512,512]{1,0:T(8,128)(2,1)S(1)} %copy-done.1, bf16[512,512]{1,0:T(8,128)(2,1)S(1)} %copy-done.2, bf16[8,128,512]{2,1,0:T(8,128)(2,1)S(1)} %get-tuple-element.11.query_ref, ...), custom_call_target="tpu_custom_call" | custom-call | flops 1073741824 | bytes 1048576 | tf_op jit(solution)/shard_map/pallas_call | solution.py:310
  39.4 7.9 %shard_map.110.sum_in = f32[8,80,512]{2,1,0:T(8,128)S(1)} custom-call(bf16[512,512]{1,0:T(8,128)(2,1)S(1)} %collective-permute-done.yes_ref.rows_ref, f32[1,512]{1,0:T(1,128)S(1)} %bitcast.12, bf16[512,512]{1,0:T(8,128)(2,1)S(1)} %copy-done.1, bf16[512,512]{1,0:T(8,128)(2,1)S(1)} %copy-done.2, bf16[8,128,512]{2,1,0:T(8,128)(2,1)S(1)} %get-tuple-element.11.query_ref, ...), custom_call_target="tpu_custom_call" | custom-call | flops 1073741824 | bytes 1048576 | tf_op jit(solution)/shard_map/pallas_call | solution.py:310
  47.3 0.0 collective-permute-done.3.rows_ref
  47.3 7.7 %shard_map.111.sum_in = f32[8,80,512]{2,1,0:T(8,128)S(1)} custom-call(bf16[512,512]{1,0:T(8,128)(2,1)S(1)} %collective-permute-done.3.rows_ref, f32[1,512]{1,0:T(1,128)S(1)} %bitcast.13, bf16[512,512]{1,0:T(8,128)(2,1)S(1)} %copy-done.1, bf16[512,512]{1,0:T(8,128)(2,1)S(1)} %copy-done.2, bf16[8,128,512]{2,1,0:T(8,128)(2,1)S(1)} %get-tuple-element.11.query_ref, ...), custom_call_target="tpu_custom_call" | custom-call | flops 1073741824 | bytes 1048576 | tf_op jit(solution)/shard_map/pallas_call | solution.py:310
  55.0 0.0 copy-start.4
  55.0 0.0 collective-permute-done.2.rows_ref
  55.0 5.3 %shard_map.112.sum_in = f32[8,80,512]{2,1,0:T(8,128)S(1)} custom-call(bf16[256,512]{1,0:T(8,128)(2,1)S(1)} %collective-permute-done.2.rows_ref, f32[1,512]{1,0:T(1,128)S(1)} %bitcast.14, bf16[512,512]{1,0:T(8,128)(2,1)S(1)} %copy-done.1, bf16[512,512]{1,0:T(8,128)(2,1)S(1)} %copy-done.2, bf16[8,128,512]{2,1,0:T(8,128)(2,1)S(1)} %get-tuple-element.11.query_ref, ...), custom_call_target="tpu_custom_call" | custom-call | flops 1073741824 | bytes 1048576 | tf_op jit(solution)/shard_map/pallas_call | solution.py:310
  60.3 0.0 copy-start.6
  60.3 0.0 copy-start.7
  60.3 0.0 copy-start.8
  60.3 0.0 collective-permute-done.1.rows_ref
  60.4 0.0 copy-done.4
  60.4 6.0 %attend_far1.1 = (f32[512,512]{1,0:T(8,128)S(1)}, f32[2,512]{1,0:T(2,128)S(1)}) custom-call(bf16[256,512]{1,0:T(8,128)(2,1)S(1)} %collective-permute-done.1.rows_ref, f32[1,512]{1,0:T(1,128)S(1)} %bitcast.15, bf16[512,512]{1,0:T(8,128)(2,1)S(1)} %copy-done.1, bf16[512,512]{1,0:T(8,128)(2,1)S(1)} %copy-done.2, ...), custom_call_target="tpu_custom_call" | custom-call | flops 1073741824 | bytes 1048576 | tf_op jit(solution)/shard_map/attend_far1/pallas_call | solution.py:319
  66.3 1.9 %collective-permute-start.5 = (f32[2,512]{1,0:T(2,128)S(1)}, f32[2,512]{1,0:T(2,128)S(1)}, u32[]{:S(2)}, u32[]{:S(2)}) collective-permute-start(f32[2,512]{1,0:T(2,128)S(1)} %get-tuple-element.16), channel_id=1, source_target_pairs={{0,1},{1,0},{2,3},{3,2},{4,5},{5,4},{6,7},{7,6},{8,9},{9,8},{10,11... | collective-permute-start | bytes 12296 | tf_op jit(solution)/shard_map/ppermute | solution.py:30
  68.3 0.8 %collective-permute-done.5 = f32[2,512]{1,0:T(2,128)S(1)} collective-permute-done((f32[2,512]{1,0:T(2,128)S(1)}, f32[2,512]{1,0:T(2,128)S(1)}, u32[]{:S(2)}, u32[]{:S(2)}) %collective-permute-start.5) | collective-permute-done | bytes 4128 | tf_op jit(solution)/shard_map/ppermute | solution.py:30
  69.1 1.1 %collective-permute-start.6 = (f32[2,512]{1,0:T(2,128)S(1)}, f32[2,512]{1,0:T(2,128)S(1)}, u32[]{:S(2)}, u32[]{:S(2)}) collective-permute-start(f32[2,512]{1,0:T(2,128)S(1)} %pad_maximum_fusion), channel_id=1, source_target_pairs={{0,8},{1,9},{2,10},{3,11},{4,12},{5,13},{6,14},{7,15},{8,0},{9,1},... | collective-permute-start | bytes 12296 | tf_op jit(solution)/shard_map/ppermute | solution.py:30
  70.2 0.8 collective-permute-start.7
  71.0 0.9 %collective-permute-start.8 = (f32[2,512]{1,0:T(2,128)S(1)}, f32[2,512]{1,0:T(2,128)S(1)}, u32[]{:S(2)}, u32[]{:S(2)}) collective-permute-start(f32[2,512]{1,0:T(2,128)S(1)} %pad_maximum_fusion), channel_id=1, source_target_pairs={{0,4},{1,13},{2,6},{3,15},{4,0},{5,9},{6,2},{7,11},{8,12},{9,5},{1... | collective-permute-start | bytes 12296 | tf_op jit(solution)/shard_map/ppermute | solution.py:30
  71.9 1.8 %collective-permute-start.9 = (f32[2,512]{1,0:T(2,128)S(1)}, f32[2,512]{1,0:T(2,128)S(1)}, u32[]{:S(2)}, u32[]{:S(2)}) collective-permute-start(f32[2,512]{1,0:T(2,128)S(1)} %pad_maximum_fusion), channel_id=1, source_target_pairs={{0,6},{1,15},{2,4},{3,13},{4,2},{5,11},{6,0},{7,9},{8,14},{9,7},{1... | collective-permute-start | bytes 12296 | tf_op jit(solution)/shard_map/ppermute | solution.py:30
  73.7 0.0 collective-permute-done.6
  73.7 0.1 collective-permute-done.7
  73.8 0.8 collective-permute-done.8
  74.6 1.8 %collective-permute-done.9 = f32[2,512]{1,0:T(2,128)S(1)} collective-permute-done((f32[2,512]{1,0:T(2,128)S(1)}, f32[2,512]{1,0:T(2,128)S(1)}, u32[]{:S(2)}, u32[]{:S(2)}) %collective-permute-start.9) | collective-permute-done | bytes 4128 | tf_op jit(solution)/shard_map/ppermute | solution.py:30
  76.5 2.0 %collective-permute-start.10 = (f32[2,512]{1,0:T(2,128)S(1)}, f32[2,512]{1,0:T(2,128)S(1)}, u32[]{:S(2)}, u32[]{:S(2)}) collective-permute-start(f32[2,512]{1,0:T(2,128)S(1)} %pad_maximum_fusion.1), channel_id=1, source_target_pairs={{0,1},{1,0},{2,3},{3,2},{4,5},{5,4},{6,7},{7,6},{8,9},{9,8},{10,11... | collective-permute-start | bytes 12296 | tf_op jit(solution)/shard_map/ppermute | solution.py:30
  78.5 0.8 %collective-permute-done.10 = f32[2,512]{1,0:T(2,128)S(1)} collective-permute-done((f32[2,512]{1,0:T(2,128)S(1)}, f32[2,512]{1,0:T(2,128)S(1)}, u32[]{:S(2)}, u32[]{:S(2)}) %collective-permute-start.10) | collective-permute-done | bytes 4128 | tf_op jit(solution)/shard_map/ppermute | solution.py:30
  79.3 0.0 copy-done
  79.3 0.0 copy-done.6
  79.3 0.0 copy-done.7
  79.4 0.0 copy-done.8
  79.4 2.2 %fusion.8 = bf16[512,512]{1,0:T(8,128)(2,1)} fusion(f32[512,512]{1,0:T(8,128)S(1)} %get-tuple-element.15, bf16[1024,512]{1,0:T(8,128)(2,1)S(1)} %copy-done, bf16[512,1024]{1,0:T(8,128)(2,1)S(1)} %copy-done.6, f32[512]{0:T(512)S(1)} %copy-done.7, f32[512]{0:T(512)S(1)} %copy-done.8, f32[512]{0:T(512)S(1)} %bitcast.17, f32[512]{0:T(512)S(1)} %bitcast.16), kind=kOutput, calls=%fused_computation.10 | convolution fusion | flops 1080295424 | bytes 3678208 | tf_op jit(solution)/shard_map/dot_general | solution.py:337
  (7 shorter events, 0.1 us)
Async XLA Ops:
  0.0 79.3 %copy-start = (bf16[1024,512]{1,0:T(8,128)(2,1)S(1)}, bf16[1024,512]{1,0:T(8,128)(2,1)}, u32[]{:S(2)}) copy-start(bf16[1024,512]{1,0:T(8,128)(2,1)} %param.21) | copy-start | bytes 3145732
  0.0 12.6 %collective-permute-start = (bf16[512,512]{1,0:T(8,128)(2,1)}, bf16[512,512]{1,0:T(8,128)(2,1)S(1)}, u32[]{:S(2)}, u32[]{:S(2)}) collective-permute-start(bf16[512,512]{1,0:T(8,128)(2,1)} %own_ref.1), channel_id=1, source_target_pairs={{0,15},{1,2},{2,1},{3,4},{4,3},{5,6},{6,5},{7,8},{8,7},{9,10},{10,... | collective-permute-start | bytes 1572872 | tf_op jit(solution)/shard_map/ppermute | solution.py:30
  5.5 26.2 %collective-permute-start.4 = (bf16[512,512]{1,0:T(8,128)(2,1)}, bf16[512,512]{1,0:T(8,128)(2,1)S(1)}, u32[]{:S(2)}, u32[]{:S(2)}) collective-permute-start(bf16[512,512]{1,0:T(8,128)(2,1)} %own_ref.1), channel_id=1, source_target_pairs={{0,1},{1,0},{2,3},{3,2},{4,5},{5,4},{6,7},{7,6},{8,9},{9,8},{10,11... | collective-permute-start | bytes 1572872 | tf_op jit(solution)/shard_map/ppermute | solution.py:30
  12.6 34.6 %collective-permute-start.3 = (bf16[512,512]{1,0:T(8,128)(2,1)S(1)}, bf16[512,512]{1,0:T(8,128)(2,1)S(1)}, u32[]{:S(2)}, u32[]{:S(2)}) collective-permute-start(bf16[512,512]{1,0:T(8,128)(2,1)S(1)} %collective-permute-done.yes_ref.rows_ref), channel_id=1, source_target_pairs={{0,1},{1,0},{2,3},{3,2},{4,5},{5,4},{6,7},{7,6},{8,9},{9,8},{10,11... | collective-permute-start | bytes 1572872 | tf_op jit(solution)/shard_map/ppermute | solution.py:30
  15.9 13.7 %copy-start.3 = (bf16[512,512]{1,0:T(8,128)(2,1)S(1)}, bf16[512,512]{1,0:T(8,128)(2,1)}, u32[]{:S(2)}) copy-start(bf16[512,512]{1,0:T(8,128)(2,1)} %own_ref.1) | copy-start | bytes 1572868
  15.9 15.8 %copy-start.1 = (bf16[512,512]{1,0:T(8,128)(2,1)S(1)}, bf16[512,512]{1,0:T(8,128)(2,1)}, u32[]{:S(2)}) copy-start(bf16[512,512]{1,0:T(8,128)(2,1)} %w_key_ref.9) | copy-start | bytes 1572868
  15.9 15.8 %copy-start.2 = (bf16[512,512]{1,0:T(8,128)(2,1)S(1)}, bf16[512,512]{1,0:T(8,128)(2,1)}, u32[]{:S(2)}) copy-start(bf16[512,512]{1,0:T(8,128)(2,1)} %w_value_ref.9) | copy-start | bytes 1572868
  15.9 15.8 %copy-start.5 = (f32[512]{0:T(512)S(1)}, f32[512]{0:T(512)}, u32[]{:S(2)}) copy-start(f32[512]{0:T(512)} %param.13) | copy-start | bytes 6148
  27.9 27.0 %collective-permute-start.2 = (bf16[256,512]{1,0:T(8,128)(2,1)S(1)}, bf16[256,512]{1,0:T(8,128)(2,1)S(1)}, u32[]{:S(2)}, u32[]{:S(2)}) collective-permute-start(bf16[256,512]{1,0:T(8,128)(2,1)S(1)} %get-tuple-element.13), channel_id=1, source_target_pairs={{0,2},{1,15},{2,4},{3,1},{4,6},{5,3},{6,8},{7,5},{8,10},{9,7},{10,... | collective-permute-start | bytes 786440 | tf_op jit(solution)/shard_map/ppermute | solution.py:30
  30.2 30.1 %collective-permute-start.1 = (bf16[256,512]{1,0:T(8,128)(2,1)S(1)}, bf16[256,512]{1,0:T(8,128)(2,1)S(1)}, u32[]{:S(2)}, u32[]{:S(2)}) collective-permute-start(bf16[256,512]{1,0:T(8,128)(2,1)S(1)} %pick_far.1), channel_id=1, source_target_pairs={{0,2},{1,4},{2,15},{3,1},{4,6},{5,8},{6,3},{7,5},{8,10},{9,12},{10... | collective-permute-start | bytes 786440 | tf_op jit(solution)/shard_map/ppermute | solution.py:30
  55.0 5.4 %copy-start.4 = (bf16[512,512]{1,0:T(8,128)(2,1)S(1)}, bf16[512,512]{1,0:T(8,128)(2,1)}, u32[]{:S(2)}) copy-start(bf16[512,512]{1,0:T(8,128)(2,1)} %w_out_ref.1) | copy-start | bytes 1572868
  60.3 19.0 %copy-start.6 = (bf16[512,1024]{1,0:T(8,128)(2,1)S(1)}, bf16[512,1024]{1,0:T(8,128)(2,1)}, u32[]{:S(2)}) copy-start(bf16[512,1024]{1,0:T(8,128)(2,1)} %param.20) | copy-start | bytes 3145732
  60.3 19.0 %copy-start.7 = (f32[512]{0:T(512)S(1)}, f32[512]{0:T(512)}, u32[]{:S(2)}) copy-start(f32[512]{0:T(512)} %param.19) | copy-start | bytes 6148
  60.3 19.0 %copy-start.8 = (f32[512]{0:T(512)S(1)}, f32[512]{0:T(512)}, u32[]{:S(2)}) copy-start(f32[512]{0:T(512)} %param.18) | copy-start | bytes 6148
  66.3 2.8 %collective-permute-start.5 = (f32[2,512]{1,0:T(2,128)S(1)}, f32[2,512]{1,0:T(2,128)S(1)}, u32[]{:S(2)}, u32[]{:S(2)}) collective-permute-start(f32[2,512]{1,0:T(2,128)S(1)} %get-tuple-element.16), channel_id=1, source_target_pairs={{0,1},{1,0},{2,3},{3,2},{4,5},{5,4},{6,7},{7,6},{8,9},{9,8},{10,11... | collective-permute-start | bytes 12296 | tf_op jit(solution)/shard_map/ppermute | solution.py:30
  69.1 4.6 %collective-permute-start.6 = (f32[2,512]{1,0:T(2,128)S(1)}, f32[2,512]{1,0:T(2,128)S(1)}, u32[]{:S(2)}, u32[]{:S(2)}) collective-permute-start(f32[2,512]{1,0:T(2,128)S(1)} %pad_maximum_fusion), channel_id=1, source_target_pairs={{0,8},{1,9},{2,10},{3,11},{4,12},{5,13},{6,14},{7,15},{8,0},{9,1},... | collective-permute-start | bytes 12296 | tf_op jit(solution)/shard_map/ppermute | solution.py:30
  70.2 3.6 %collective-permute-start.7 = (f32[2,512]{1,0:T(2,128)S(1)}, f32[2,512]{1,0:T(2,128)S(1)}, u32[]{:S(2)}, u32[]{:S(2)}) collective-permute-start(f32[2,512]{1,0:T(2,128)S(1)} %pad_maximum_fusion), channel_id=1, source_target_pairs={{0,2},{1,11},{2,0},{3,9},{4,6},{5,15},{6,4},{7,13},{8,10},{9,3},{1... | collective-permute-start | bytes 12296 | tf_op jit(solution)/shard_map/ppermute | solution.py:30
  71.0 3.6 %collective-permute-start.8 = (f32[2,512]{1,0:T(2,128)S(1)}, f32[2,512]{1,0:T(2,128)S(1)}, u32[]{:S(2)}, u32[]{:S(2)}) collective-permute-start(f32[2,512]{1,0:T(2,128)S(1)} %pad_maximum_fusion), channel_id=1, source_target_pairs={{0,4},{1,13},{2,6},{3,15},{4,0},{5,9},{6,2},{7,11},{8,12},{9,5},{1... | collective-permute-start | bytes 12296 | tf_op jit(solution)/shard_map/ppermute | solution.py:30
  71.9 4.5 %collective-permute-start.9 = (f32[2,512]{1,0:T(2,128)S(1)}, f32[2,512]{1,0:T(2,128)S(1)}, u32[]{:S(2)}, u32[]{:S(2)}) collective-permute-start(f32[2,512]{1,0:T(2,128)S(1)} %pad_maximum_fusion), channel_id=1, source_target_pairs={{0,6},{1,15},{2,4},{3,13},{4,2},{5,11},{6,0},{7,9},{8,14},{9,7},{1... | collective-permute-start | bytes 12296 | tf_op jit(solution)/shard_map/ppermute | solution.py:30
  76.5 2.8 %collective-permute-start.10 = (f32[2,512]{1,0:T(2,128)S(1)}, f32[2,512]{1,0:T(2,128)S(1)}, u32[]{:S(2)}, u32[]{:S(2)}) collective-permute-start(f32[2,512]{1,0:T(2,128)S(1)} %pad_maximum_fusion.1), channel_id=1, source_target_pairs={{0,1},{1,0},{2,3},{3,2},{4,5},{5,4},{6,7},{7,6},{8,9},{9,8},{10,11... | collective-permute-start | bytes 12296 | tf_op jit(solution)/shard_map/ppermute | solution.py:30

commit v2 on v1

--- a/solution.py
+++ b/solution.py
@@ -63,7 +63,7 @@
     return jnp.transpose(bias).astype(F32)
 
 
-def attend(rows, gain, w_key, w_value, query_ref, bias_ref, keep, work, old, new):
+def attend(rows, gain, w_key, w_value, query_ref, bias_ref, keep, work, old, new, finish=None):
     keys_ref, values_ref = work
     slot, first = keep
     count, tile = rows.shape[0], bias_ref.shape[-1]
@@ -80,8 +80,8 @@
     def mix(head, weight):
         return jnp.dot(values_ref[head], weight.astype(BF16), preferred_element_type=F32)
 
+    fill_values(normed, w_value, values_ref)
     pending = [raw(head) for head in range(ahead)]
-    fill_values(normed, w_value, values_ref)
     strayed = jnp.zeros((ROWS, tile), F32)
     for head in range(HEADS):
         if head + ahead < HEADS:
@@ -93,6 +93,9 @@
         total, shift = mixed[TOTAL:SHIFT], mixed[SHIFT:]
         fits = (total <= LIMIT) & (total >= 1.0 / LIMIT) & (shift == 0.0)
         strayed = jnp.where(fits, strayed, 1.0)
+
+    if finish is not None:
+        finish()
 
     @pl.when(jnp.max(strayed) > 0.0)
     def _():
@@ -110,11 +113,13 @@
             return carry
 
         lax.fori_loop(0, HEADS, one_head, 0)
+        if finish is not None:
+            finish()
 
 
 def first_kernel(
     which_ref, own_hbm, mask_hbm, gain_hbm, w_query_hbm, w_key_hbm, w_value_hbm,
-    query_ref, bias_ref, sum_ref, piece_ref,
+    query_ref, bias_ref, sum_ref, piece_ref, flag_ref,
     own_ref, mask_ref, gain_ref, w_query_ref, w_key_ref, w_value_ref,
     keys_ref, values_ref, sems,
 ):
@@ -133,6 +138,7 @@
     ]
     for fetch in fetches:
         fetch.start()
+    flag_ref[...] = jnp.full(flag_ref.shape, which_ref[WIDTHS], jnp.int32)
     fetches[0].wait()
     piece_ref[...] = own_ref[: piece_ref.shape[0], :]
     fetches[1].wait()
@@ -172,35 +178,35 @@
     own_ref, w_out_ref, after_ref, stats_ref,
     keys_ref, values_ref, sum_ref, *, slot, first,
 ):
-    next_kernel(
-        rows_ref, gain_ref, w_key_ref, w_value_ref, query_ref, bias_ref, sum_in,
-        sum_ref, keys_ref, values_ref, slot=slot, first=first,
-    )
-    mixed_t = jnp.concatenate(
-        [
-            (sum_ref[head, :HEAD_DIM] * (1.0 / sum_ref[head, TOTAL : TOTAL + 1])).astype(BF16)
-            for head in range(HEADS)
-        ],
-        axis=0,
-    )
-    mixed = jnp.transpose(mixed_t)
-    after = own_ref[...].astype(F32) + jnp.dot(
-        mixed, w_out_ref[...], preferred_element_type=F32
-    )
-    after_ref[...] = after
-    mean = jnp.mean(after, axis=0, keepdims=True)
-    centered = after - mean
-    stats_ref[0:1, :] = mean
-    stats_ref[1:2, :] = jnp.sum(centered * centered, axis=0, keepdims=True)
+    def finish():
+        mixed_t = jnp.concatenate(
+            [
+                (sum_ref[head, :HEAD_DIM] * (1.0 / sum_ref[head, TOTAL : TOTAL + 1])).astype(BF16)
+                for head in range(HEADS)
+            ],
+            axis=0,
+        )
+        mixed = jnp.transpose(mixed_t)
+        after = own_ref[...].astype(F32) + jnp.dot(
+            mixed, w_out_ref[...], preferred_element_type=F32
+        )
+        after_ref[...] = after
+        mean = jnp.mean(after, axis=0, keepdims=True)
+        centered = after - mean
+        stats_ref[0:1, :] = mean
+        stats_ref[1:2, :] = jnp.sum(centered * centered, axis=0, keepdims=True)
+
+    attend(
+        rows_ref[...], gain_ref[...], w_key_ref[...], w_value_ref[...], query_ref, bias_ref,
+        (slot, first), (keys_ref, values_ref), sum_in, sum_ref, finish,
+    )
 
 
 def pick_kernel(flag_ref, yes_ref, no_ref, out_ref):
     first = yes_ref.shape[0] - out_ref.shape[0]
-    for value, source in ((1, yes_ref), (0, no_ref)):
-
-        @pl.when(flag_ref[WIDTHS] == value)
-        def _():
-            out_ref[...] = source[first:, :]
+    out_ref[...] = jnp.where(
+        flag_ref[...] > 0, yes_ref[first:, :].astype(F32), no_ref[first:, :].astype(F32)
+    ).astype(BF16)
 
 
 def joined(parts, rows):
@@ -211,6 +217,10 @@
 
 def merged(stats, rows, axis):
     count = lax.axis_size(axis)
+    if count & (count - 1):
+        every = lax.all_gather(stats, axis)
+        stats = joined([every[place] for place in range(count)], rows)
+        return stats[0], stats[1] / (count * rows)
     step = 1
     while step < count:
         if count % (16 * step) == 0 and step == 1:
@@ -236,9 +246,9 @@
     tile, width = atoms.shape
     place = lax.axis_index("blk") % 4
     sign = 1 - 2 * (place % 2)
-    inner = (place + 1) // 2 % 2
     which = jnp.stack(
-        [REACH + 0 * sign, REACH + sign, REACH - sign, REACH + 2 * sign, REACH - 2 * sign, inner]
+        [REACH + 0 * sign, REACH + sign, REACH - sign, REACH + 2 * sign, REACH - 2 * sign]
+        + [(place + 1) // 2 % 2]
     )
     across = moved(atoms, "blk", lambda s: s + 1 if s % 2 else s - 1)
     mate = moved(atoms, "blk", lambda s: s ^ 1)
@@ -255,7 +265,6 @@
             pltpu.VMEM((HEADS, DEPTH, rows), BF16),
         ]
 
-
     def params(mib):
         return pltpu.CompilerParams(vmem_limit_bytes=mib * 1024 * 1024)
 
@@ -265,25 +274,16 @@
 
     passed = moved(across, "blk", lambda s: s ^ 1)
     half = tile // 2
-    forward = pl.pallas_call(
-        pick_kernel,
-        in_specs=[smem, vmem, vmem],
-        out_specs=vmem,
-        out_shape=jax.ShapeDtypeStruct((half, width), BF16),
-        compiler_params=params(2),
-        name="pick_far",
-    )(which, across, atoms)
-    far1 = moved(forward, "blk", lambda s: s + (2, 3, -3, -2)[s % 4])
-
-    query_heads, bias, sums, piece = pl.pallas_call(
+    query_heads, bias, sums, piece, inner = pl.pallas_call(
         first_kernel,
         in_specs=[smem] + [hbm] * 6,
-        out_specs=[vmem] * 4,
+        out_specs=[vmem] * 5,
         out_shape=[
             jax.ShapeDtypeStruct((HEADS, PAIR, tile), BF16),
             jax.ShapeDtypeStruct((WIDTHS, tile, tile), F32),
             state,
             jax.ShapeDtypeStruct((half, width), BF16),
+            jax.ShapeDtypeStruct((1, width), jnp.int32),
         ],
         scratch_shapes=[
             pltpu.VMEM((tile, width), BF16),
@@ -306,6 +306,15 @@
         ),
     )
     far0 = moved(piece, "blk", lambda s: s - 2 if s % 2 else s + 2)
+    forward = pl.pallas_call(
+        pick_kernel,
+        in_specs=[vmem] * 3,
+        out_specs=vmem,
+        out_shape=jax.ShapeDtypeStruct((half, width), BF16),
+        compiler_params=params(2),
+        name="pick_far",
+    )(inner, across, atoms)
+    far1 = moved(forward, "blk", lambda s: s + (2, 3, -3, -2)[s % 4])
     for rows, slot in ((mate, 1), (across, 2), (passed, 3), (far0, 4)):
         sums = pl.pallas_call(
             functools.partial(next_kernel, slot=slot),

time: 81.8 us -> 81.5 us (level)
  no operation moved by 1% of the time
where the time goes in v2:
time: 81.5 us; the launch traced here: 81.3 us
  Pallas kernels  46.8 us (57%)
  starting transfers between devices  20.4 us (25%)
  waiting for transfers between devices  11.5 us (14%)
  matrix products  2.25 us (3%)
    pallas_call x4, Pallas kernels, body(): pl.pallas_call(functools.partial(next_kernel, slot=slot), in_specs=[vmem]...  28.3 us
    ppermute x11, starting transfers between devices, moved(): return lax.ppermute(value, axis, pairs)  20.4 us
    pallas_call x1, Pallas kernels, body(): pl.pallas_call(first_kernel, in_specs=[smem] + [hbm] * 6, out_specs=[vmem...  12.2 us
    ppermute x11, waiting for transfers between devices, moved(): return lax.ppermute(value, axis, pairs)  11.5 us
    pallas_call x1, Pallas kernels, body(): pl.pallas_call(functools.partial(last_kernel, slot=WIDTHS - 1, first=half...  6.23 us
    dot_general x1, matrix products, body(): jnp.dot(hidden, w_down, preferred_element_type=F32)  2.25 us
  transfers between devices with their start and end apart: 11, of which 6 were waited for; matrix products, arithmetic and copies ran while one was open for 0% of the time, Pallas kernels for 50%

profile of v2, /device:TPU:0, one launch (start us, length us, event | category | flops | bytes accessed | tf_op | source)
XLA Modules:
  0.0 81.3 jit_solution(14133413790127176982)
XLA Ops:
  0.0 0.0 copy-start
  0.0 5.5 %collective-permute-start = (bf16[512,512]{1,0:T(8,128)(2,1)}, bf16[512,512]{1,0:T(8,128)(2,1)S(1)}, u32[]{:S(2)}, u32[]{:S(2)}) collective-permute-start(bf16[512,512]{1,0:T(8,128)(2,1)} %own_ref.1), channel_id=1, source_target_pairs={{0,15},{1,2},{2,1},{3,4},{4,3},{5,6},{6,5},{7,8},{8,7},{9,10},{10,... | collective-permute-start | bytes 1572872 | tf_op jit(solution)/shard_map/ppermute | solution.py:30
  5.5 0.0 collective-permute-start.4
  5.5 7.2 %collective-permute-done.yes_ref.rows_ref = bf16[512,512]{1,0:T(8,128)(2,1)S(1)} collective-permute-done((bf16[512,512]{1,0:T(8,128)(2,1)}, bf16[512,512]{1,0:T(8,128)(2,1)S(1)}, u32[]{:S(2)}, u32[]{:S(2)}) %collective-permute-start) | collective-permute-done | bytes 524320 | tf_op jit(solution)/shard_map/ppermute | solution.py:30
  12.6 3.2 %collective-permute-start.3 = (bf16[512,512]{1,0:T(8,128)(2,1)S(1)}, bf16[512,512]{1,0:T(8,128)(2,1)S(1)}, u32[]{:S(2)}, u32[]{:S(2)}) collective-permute-start(bf16[512,512]{1,0:T(8,128)(2,1)S(1)} %collective-permute-done.yes_ref.rows_ref), channel_id=1, source_target_pairs={{0,1},{1,0},{2,3},{3,2},{4,5},{5,4},{6,7},{7,6},{8,9},{9,8},{10,11... | collective-permute-start | bytes 1572872 | tf_op jit(solution)/shard_map/ppermute | solution.py:30
  15.8 0.1 stack.34.which_ref
  15.9 0.0 copy-start.3
  15.9 0.0 copy-start.1
  15.9 0.0 copy-start.5
  15.9 12.2 %attend_own.1 = (bf16[8,128,512]{2,1,0:T(8,128)(2,1)S(1)}, f32[5,512,512]{2,1,0:T(8,128)S(1)}, f32[8,80,512]{2,1,0:T(8,128)S(1)}, bf16[256,512]{1,0:T(8,128)(2,1)S(1)}, s32[1,512]{1,0:T(1,128)S(1)}) custom-call(s32[6]{0:T(128)S(1)} %stack.34.which_ref, bf16[512,512]{1,0:T(8,128)(2,1)} %own_ref.1, s32[1,5,512,512]{3,2,1,0:T(8,128)} %mask_hbm.1, ...), custom_call_target="tpu_custom_call" | custom-call | flops 1073741824 | bytes 1048576 | tf_op jit(solution)/shard_map/attend_own/pallas_call | solution.py:277
  28.1 1.7 %collective-permute-start.2 = (bf16[256,512]{1,0:T(8,128)(2,1)S(1)}, bf16[256,512]{1,0:T(8,128)(2,1)S(1)}, u32[]{:S(2)}, u32[]{:S(2)}) collective-permute-start(bf16[256,512]{1,0:T(8,128)(2,1)S(1)} %get-tuple-element.15), channel_id=1, source_target_pairs={{0,2},{1,15},{2,4},{3,1},{4,6},{5,3},{6,8},{7,5},{8,10},{9,7},{10,... | collective-permute-start | bytes 786440 | tf_op jit(solution)/shard_map/ppermute | solution.py:30
  29.8 0.0 copy-done.3
  29.8 0.1 pick_far.1
  29.9 1.5 %collective-permute-start.1 = (bf16[256,512]{1,0:T(8,128)(2,1)S(1)}, bf16[256,512]{1,0:T(8,128)(2,1)S(1)}, u32[]{:S(2)}, u32[]{:S(2)}) collective-permute-start(bf16[256,512]{1,0:T(8,128)(2,1)S(1)} %pick_far.1), channel_id=1, source_target_pairs={{0,2},{1,4},{2,15},{3,1},{4,6},{5,8},{6,3},{7,5},{8,10},{9,12},{10... | collective-permute-start | bytes 786440 | tf_op jit(solution)/shard_map/ppermute | solution.py:30
  31.3 0.0 collective-permute-done.4.rows_ref
  31.3 0.0 copy-done.1
  31.3 0.0 copy-done.2
  31.4 0.0 copy-done.5
  31.4 7.7 %shard_map.109.sum_in = f32[8,80,512]{2,1,0:T(8,128)S(1)} custom-call(bf16[512,512]{1,0:T(8,128)(2,1)S(1)} %collective-permute-done.4.rows_ref, f32[1,512]{1,0:T(1,128)S(1)} %bitcast.11, bf16[512,512]{1,0:T(8,128)(2,1)S(1)} %copy-done.1, bf16[512,512]{1,0:T(8,128)(2,1)S(1)} %copy-done.2, bf16[8,128,512]{2,1,0:T(8,128)(2,1)S(1)} %get-tuple-element.13.query_ref, ...), custom_call_target="tpu_custom_call" | custom-call | flops 1073741824 | bytes 1048576 | tf_op jit(solution)/shard_map/pallas_call | solution.py:319
  39.0 7.9 %shard_map.110.sum_in = f32[8,80,512]{2,1,0:T(8,128)S(1)} custom-call(bf16[512,512]{1,0:T(8,128)(2,1)S(1)} %collective-permute-done.yes_ref.rows_ref, f32[1,512]{1,0:T(1,128)S(1)} %bitcast.12, bf16[512,512]{1,0:T(8,128)(2,1)S(1)} %copy-done.1, bf16[512,512]{1,0:T(8,128)(2,1)S(1)} %copy-done.2, bf16[8,128,512]{2,1,0:T(8,128)(2,1)S(1)} %get-tuple-element.13.query_ref, ...), custom_call_target="tpu_custom_call" | custom-call | flops 1073741824 | bytes 1048576 | tf_op jit(solution)/shard_map/pallas_call | solution.py:319
  46.9 0.0 collective-permute-done.3.rows_ref
  46.9 7.7 %shard_map.111.sum_in = f32[8,80,512]{2,1,0:T(8,128)S(1)} custom-call(bf16[512,512]{1,0:T(8,128)(2,1)S(1)} %collective-permute-done.3.rows_ref, f32[1,512]{1,0:T(1,128)S(1)} %bitcast.13, bf16[512,512]{1,0:T(8,128)(2,1)S(1)} %copy-done.1, bf16[512,512]{1,0:T(8,128)(2,1)S(1)} %copy-done.2, bf16[8,128,512]{2,1,0:T(8,128)(2,1)S(1)} %get-tuple-element.13.query_ref, ...), custom_call_target="tpu_custom_call" | custom-call | flops 1073741824 | bytes 1048576 | tf_op jit(solution)/shard_map/pallas_call | solution.py:319
  54.6 0.0 copy-start.4
  54.6 0.0 collective-permute-done.2.rows_ref
  54.6 5.1 %shard_map.112.sum_in = f32[8,80,512]{2,1,0:T(8,128)S(1)} custom-call(bf16[256,512]{1,0:T(8,128)(2,1)S(1)} %collective-permute-done.2.rows_ref, f32[1,512]{1,0:T(1,128)S(1)} %bitcast.14, bf16[512,512]{1,0:T(8,128)(2,1)S(1)} %copy-done.1, bf16[512,512]{1,0:T(8,128)(2,1)S(1)} %copy-done.2, bf16[8,128,512]{2,1,0:T(8,128)(2,1)S(1)} %get-tuple-element.13.query_ref, ...), custom_call_target="tpu_custom_call" | custom-call | flops 1073741824 | bytes 1048576 | tf_op jit(solution)/shard_map/pallas_call | solution.py:319
  59.7 0.0 copy-start.6
  59.7 0.0 copy-start.7
  59.7 0.0 copy-start.8
  59.8 0.0 collective-permute-done.1.rows_ref
  59.8 0.0 copy-done.4
  59.8 6.2 %attend_far1.1 = (f32[512,512]{1,0:T(8,128)S(1)}, f32[2,512]{1,0:T(2,128)S(1)}) custom-call(bf16[256,512]{1,0:T(8,128)(2,1)S(1)} %collective-permute-done.1.rows_ref, f32[1,512]{1,0:T(1,128)S(1)} %bitcast.15, bf16[512,512]{1,0:T(8,128)(2,1)S(1)} %copy-done.1, bf16[512,512]{1,0:T(8,128)(2,1)S(1)} %copy-done.2, ...), custom_call_target="tpu_custom_call" | custom-call | flops 1073741824 | bytes 1048576 | tf_op jit(solution)/shard_map/attend_far1/pallas_call | solution.py:328
  66.0 2.0 %collective-permute-start.5 = (f32[2,512]{1,0:T(2,128)S(1)}, f32[2,512]{1,0:T(2,128)S(1)}, u32[]{:S(2)}, u32[]{:S(2)}) collective-permute-start(f32[2,512]{1,0:T(2,128)S(1)} %get-tuple-element.18), channel_id=1, source_target_pairs={{0,1},{1,0},{2,3},{3,2},{4,5},{5,4},{6,7},{7,6},{8,9},{9,8},{10,11... | collective-permute-start | bytes 12296 | tf_op jit(solution)/shard_map/ppermute | solution.py:30
  68.0 0.8 %collective-permute-done.5 = f32[2,512]{1,0:T(2,128)S(1)} collective-permute-done((f32[2,512]{1,0:T(2,128)S(1)}, f32[2,512]{1,0:T(2,128)S(1)}, u32[]{:S(2)}, u32[]{:S(2)}) %collective-permute-start.5) | collective-permute-done | bytes 4128 | tf_op jit(solution)/shard_map/ppermute | solution.py:30
  68.8 1.1 %collective-permute-start.6 = (f32[2,512]{1,0:T(2,128)S(1)}, f32[2,512]{1,0:T(2,128)S(1)}, u32[]{:S(2)}, u32[]{:S(2)}) collective-permute-start(f32[2,512]{1,0:T(2,128)S(1)} %pad_maximum_fusion), channel_id=1, source_target_pairs={{0,8},{1,9},{2,10},{3,11},{4,12},{5,13},{6,14},{7,15},{8,0},{9,1},... | collective-permute-start | bytes 12296 | tf_op jit(solution)/shard_map/ppermute | solution.py:30
  69.9 0.8 collective-permute-start.7
  70.7 0.9 %collective-permute-start.8 = (f32[2,512]{1,0:T(2,128)S(1)}, f32[2,512]{1,0:T(2,128)S(1)}, u32[]{:S(2)}, u32[]{:S(2)}) collective-permute-start(f32[2,512]{1,0:T(2,128)S(1)} %pad_maximum_fusion), channel_id=1, source_target_pairs={{0,4},{1,13},{2,6},{3,15},{4,0},{5,9},{6,2},{7,11},{8,12},{9,5},{1... | collective-permute-start | bytes 12296 | tf_op jit(solution)/shard_map/ppermute | solution.py:30
  71.6 1.8 %collective-permute-start.9 = (f32[2,512]{1,0:T(2,128)S(1)}, f32[2,512]{1,0:T(2,128)S(1)}, u32[]{:S(2)}, u32[]{:S(2)}) collective-permute-start(f32[2,512]{1,0:T(2,128)S(1)} %pad_maximum_fusion), channel_id=1, source_target_pairs={{0,6},{1,15},{2,4},{3,13},{4,2},{5,11},{6,0},{7,9},{8,14},{9,7},{1... | collective-permute-start | bytes 12296 | tf_op jit(solution)/shard_map/ppermute | solution.py:30
  73.4 0.0 collective-permute-done.6
  73.4 0.1 collective-permute-done.7
  73.5 0.8 collective-permute-done.8
  74.3 1.8 %collective-permute-done.9 = f32[2,512]{1,0:T(2,128)S(1)} collective-permute-done((f32[2,512]{1,0:T(2,128)S(1)}, f32[2,512]{1,0:T(2,128)S(1)}, u32[]{:S(2)}, u32[]{:S(2)}) %collective-permute-start.9) | collective-permute-done | bytes 4128 | tf_op jit(solution)/shard_map/ppermute | solution.py:30
  76.2 2.0 %collective-permute-start.10 = (f32[2,512]{1,0:T(2,128)S(1)}, f32[2,512]{1,0:T(2,128)S(1)}, u32[]{:S(2)}, u32[]{:S(2)}) collective-permute-start(f32[2,512]{1,0:T(2,128)S(1)} %pad_maximum_fusion.1), channel_id=1, source_target_pairs={{0,1},{1,0},{2,3},{3,2},{4,5},{5,4},{6,7},{7,6},{8,9},{9,8},{10,11... | collective-permute-start | bytes 12296 | tf_op jit(solution)/shard_map/ppermute | solution.py:30
  78.2 0.8 %collective-permute-done.10 = f32[2,512]{1,0:T(2,128)S(1)} collective-permute-done((f32[2,512]{1,0:T(2,128)S(1)}, f32[2,512]{1,0:T(2,128)S(1)}, u32[]{:S(2)}, u32[]{:S(2)}) %collective-permute-start.10) | collective-permute-done | bytes 4128 | tf_op jit(solution)/shard_map/ppermute | solution.py:30
  79.0 0.0 copy-done
  79.0 0.0 copy-done.6
  79.0 0.0 copy-done.7
  79.1 0.0 copy-done.8
  79.1 2.2 %fusion.8 = bf16[512,512]{1,0:T(8,128)(2,1)} fusion(f32[512,512]{1,0:T(8,128)S(1)} %get-tuple-element.17, bf16[1024,512]{1,0:T(8,128)(2,1)S(1)} %copy-done, bf16[512,1024]{1,0:T(8,128)(2,1)S(1)} %copy-done.6, f32[512]{0:T(512)S(1)} %copy-done.7, f32[512]{0:T(512)S(1)} %copy-done.8, f32[512]{0:T(512)S(1)} %bitcast.17, f32[512]{0:T(512)S(1)} %bitcast.16), kind=kOutput, calls=%fused_computation.10 | convolution fusion | flops 1080295424 | bytes 3678208 | tf_op jit(solution)/shard_map/dot_general | solution.py:346
  (7 shorter events, 0.1 us)
Async XLA Ops:
  0.0 79.0 %copy-start = (bf16[1024,512]{1,0:T(8,128)(2,1)S(1)}, bf16[1024,512]{1,0:T(8,128)(2,1)}, u32[]{:S(2)}) copy-start(bf16[1024,512]{1,0:T(8,128)(2,1)} %param.21) | copy-start | bytes 3145732
  0.0 12.6 %collective-permute-start = (bf16[512,512]{1,0:T(8,128)(2,1)}, bf16[512,512]{1,0:T(8,128)(2,1)S(1)}, u32[]{:S(2)}, u32[]{:S(2)}) collective-permute-start(bf16[512,512]{1,0:T(8,128)(2,1)} %own_ref.1), channel_id=1, source_target_pairs={{0,15},{1,2},{2,1},{3,4},{4,3},{5,6},{6,5},{7,8},{8,7},{9,10},{10,... | collective-permute-start | bytes 1572872 | tf_op jit(solution)/shard_map/ppermute | solution.py:30
  5.5 25.9 %collective-permute-start.4 = (bf16[512,512]{1,0:T(8,128)(2,1)}, bf16[512,512]{1,0:T(8,128)(2,1)S(1)}, u32[]{:S(2)}, u32[]{:S(2)}) collective-permute-start(bf16[512,512]{1,0:T(8,128)(2,1)} %own_ref.1), channel_id=1, source_target_pairs={{0,1},{1,0},{2,3},{3,2},{4,5},{5,4},{6,7},{7,6},{8,9},{9,8},{10,11... | collective-permute-start | bytes 1572872 | tf_op jit(solution)/shard_map/ppermute | solution.py:30
  12.6 34.3 %collective-permute-start.3 = (bf16[512,512]{1,0:T(8,128)(2,1)S(1)}, bf16[512,512]{1,0:T(8,128)(2,1)S(1)}, u32[]{:S(2)}, u32[]{:S(2)}) collective-permute-start(bf16[512,512]{1,0:T(8,128)(2,1)S(1)} %collective-permute-done.yes_ref.rows_ref), channel_id=1, source_target_pairs={{0,1},{1,0},{2,3},{3,2},{4,5},{5,4},{6,7},{7,6},{8,9},{9,8},{10,11... | collective-permute-start | bytes 1572872 | tf_op jit(solution)/shard_map/ppermute | solution.py:30
  15.9 13.9 %copy-start.3 = (bf16[512,512]{1,0:T(8,128)(2,1)S(1)}, bf16[512,512]{1,0:T(8,128)(2,1)}, u32[]{:S(2)}) copy-start(bf16[512,512]{1,0:T(8,128)(2,1)} %own_ref.1) | copy-start | bytes 1572868
  15.9 15.5 %copy-start.1 = (bf16[512,512]{1,0:T(8,128)(2,1)S(1)}, bf16[512,512]{1,0:T(8,128)(2,1)}, u32[]{:S(2)}) copy-start(bf16[512,512]{1,0:T(8,128)(2,1)} %w_key_ref.9) | copy-start | bytes 1572868
  15.9 15.5 %copy-start.2 = (bf16[512,512]{1,0:T(8,128)(2,1)S(1)}, bf16[512,512]{1,0:T(8,128)(2,1)}, u32[]{:S(2)}) copy-start(bf16[512,512]{1,0:T(8,128)(2,1)} %w_value_ref.9) | copy-start | bytes 1572868
  15.9 15.5 %copy-start.5 = (f32[512]{0:T(512)S(1)}, f32[512]{0:T(512)}, u32[]{:S(2)}) copy-start(f32[512]{0:T(512)} %param.13) | copy-start | bytes 6148
  28.1 26.5 %collective-permute-start.2 = (bf16[256,512]{1,0:T(8,128)(2,1)S(1)}, bf16[256,512]{1,0:T(8,128)(2,1)S(1)}, u32[]{:S(2)}, u32[]{:S(2)}) collective-permute-start(bf16[256,512]{1,0:T(8,128)(2,1)S(1)} %get-tuple-element.15), channel_id=1, source_target_pairs={{0,2},{1,15},{2,4},{3,1},{4,6},{5,3},{6,8},{7,5},{8,10},{9,7},{10,... | collective-permute-start | bytes 786440 | tf_op jit(solution)/shard_map/ppermute | solution.py:30
  29.9 29.9 %collective-permute-start.1 = (bf16[256,512]{1,0:T(8,128)(2,1)S(1)}, bf16[256,512]{1,0:T(8,128)(2,1)S(1)}, u32[]{:S(2)}, u32[]{:S(2)}) collective-permute-start(bf16[256,512]{1,0:T(8,128)(2,1)S(1)} %pick_far.1), channel_id=1, source_target_pairs={{0,2},{1,4},{2,15},{3,1},{4,6},{5,8},{6,3},{7,5},{8,10},{9,12},{10... | collective-permute-start | bytes 786440 | tf_op jit(solution)/shard_map/ppermute | solution.py:30
  54.6 5.2 %copy-start.4 = (bf16[512,512]{1,0:T(8,128)(2,1)S(1)}, bf16[512,512]{1,0:T(8,128)(2,1)}, u32[]{:S(2)}) copy-start(bf16[512,512]{1,0:T(8,128)(2,1)} %w_out_ref.1) | copy-start | bytes 1572868
  59.7 19.3 %copy-start.6 = (bf16[512,1024]{1,0:T(8,128)(2,1)S(1)}, bf16[512,1024]{1,0:T(8,128)(2,1)}, u32[]{:S(2)}) copy-start(bf16[512,1024]{1,0:T(8,128)(2,1)} %param.20) | copy-start | bytes 3145732
  59.7 19.3 %copy-start.7 = (f32[512]{0:T(512)S(1)}, f32[512]{0:T(512)}, u32[]{:S(2)}) copy-start(f32[512]{0:T(512)} %param.19) | copy-start | bytes 6148
  59.7 19.3 %copy-start.8 = (f32[512]{0:T(512)S(1)}, f32[512]{0:T(512)}, u32[]{:S(2)}) copy-start(f32[512]{0:T(512)} %param.18) | copy-start | bytes 6148
  66.0 2.8 %collective-permute-start.5 = (f32[2,512]{1,0:T(2,128)S(1)}, f32[2,512]{1,0:T(2,128)S(1)}, u32[]{:S(2)}, u32[]{:S(2)}) collective-permute-start(f32[2,512]{1,0:T(2,128)S(1)} %get-tuple-element.18), channel_id=1, source_target_pairs={{0,1},{1,0},{2,3},{3,2},{4,5},{5,4},{6,7},{7,6},{8,9},{9,8},{10,11... | collective-permute-start | bytes 12296 | tf_op jit(solution)/shard_map/ppermute | solution.py:30
  68.8 4.6 %collective-permute-start.6 = (f32[2,512]{1,0:T(2,128)S(1)}, f32[2,512]{1,0:T(2,128)S(1)}, u32[]{:S(2)}, u32[]{:S(2)}) collective-permute-start(f32[2,512]{1,0:T(2,128)S(1)} %pad_maximum_fusion), channel_id=1, source_target_pairs={{0,8},{1,9},{2,10},{3,11},{4,12},{5,13},{6,14},{7,15},{8,0},{9,1},... | collective-permute-start | bytes 12296 | tf_op jit(solution)/shard_map/ppermute | solution.py:30
  69.9 3.6 %collective-permute-start.7 = (f32[2,512]{1,0:T(2,128)S(1)}, f32[2,512]{1,0:T(2,128)S(1)}, u32[]{:S(2)}, u32[]{:S(2)}) collective-permute-start(f32[2,512]{1,0:T(2,128)S(1)} %pad_maximum_fusion), channel_id=1, source_target_pairs={{0,2},{1,11},{2,0},{3,9},{4,6},{5,15},{6,4},{7,13},{8,10},{9,3},{1... | collective-permute-start | bytes 12296 | tf_op jit(solution)/shard_map/ppermute | solution.py:30
  70.7 3.6 %collective-permute-start.8 = (f32[2,512]{1,0:T(2,128)S(1)}, f32[2,512]{1,0:T(2,128)S(1)}, u32[]{:S(2)}, u32[]{:S(2)}) collective-permute-start(f32[2,512]{1,0:T(2,128)S(1)} %pad_maximum_fusion), channel_id=1, source_target_pairs={{0,4},{1,13},{2,6},{3,15},{4,0},{5,9},{6,2},{7,11},{8,12},{9,5},{1... | collective-permute-start | bytes 12296 | tf_op jit(solution)/shard_map/ppermute | solution.py:30
  71.6 4.5 %collective-permute-start.9 = (f32[2,512]{1,0:T(2,128)S(1)}, f32[2,512]{1,0:T(2,128)S(1)}, u32[]{:S(2)}, u32[]{:S(2)}) collective-permute-start(f32[2,512]{1,0:T(2,128)S(1)} %pad_maximum_fusion), channel_id=1, source_target_pairs={{0,6},{1,15},{2,4},{3,13},{4,2},{5,11},{6,0},{7,9},{8,14},{9,7},{1... | collective-permute-start | bytes 12296 | tf_op jit(solution)/shard_map/ppermute | solution.py:30
  76.2 2.8 %collective-permute-start.10 = (f32[2,512]{1,0:T(2,128)S(1)}, f32[2,512]{1,0:T(2,128)S(1)}, u32[]{:S(2)}, u32[]{:S(2)}) collective-permute-start(f32[2,512]{1,0:T(2,128)S(1)} %pad_maximum_fusion.1), channel_id=1, source_target_pairs={{0,1},{1,0},{2,3},{3,2},{4,5},{5,4},{6,7},{7,6},{8,9},{9,8},{10,11... | collective-permute-start | bytes 12296 | tf_op jit(solution)/shard_map/ppermute | solution.py:30

commit v3 on v2

--- a/solution.py
+++ b/solution.py
@@ -20,6 +20,7 @@
 BLOCKED = -1e30
 LOG2E = 1.4426950408889634
 LIMIT = 2.0**80
+GELU = 0.7978845608028654
 F32 = jnp.float32
 BF16 = jnp.bfloat16
 
@@ -202,6 +203,43 @@
     )
 
 
+def forward_kernel(
+    after_ref, mine_ref, other_ref, gain_ref, shift_ref, w_up_ref, w_down_ref, out_hbm, out_ref, sems,
+    *, count,
+):
+    rows = out_ref.shape[0] // sems.shape[0]
+    mean = 0.5 * (mine_ref[0:1, :] + other_ref[0:1, :])
+    gap = mine_ref[0:1, :] - other_ref[0:1, :]
+    var = (mine_ref[1:2, :] + other_ref[1:2, :]) * (1.0 / count) + 0.25 * gap * gap
+    scale = lax.rsqrt(var + 1e-05) * gain_ref[...]
+
+    def up(part):
+        after = after_ref[part * rows : (part + 1) * rows, :]
+        batched = ((after - mean) * scale + shift_ref[...]).astype(BF16)
+        return jnp.dot(batched, w_up_ref[...], preferred_element_type=F32)
+
+    copies = []
+    raw = up(0)
+    for part in range(sems.shape[0]):
+        current = raw
+        if part + 1 < sems.shape[0]:
+            raw = up(part + 1)
+        inner = current * (GELU + (GELU * 0.044715) * (current * current))
+        halved = 0.5 * current
+        hidden = (halved + halved * jnp.tanh(inner)).astype(BF16)
+        block = pl.ds(part * rows, rows)
+        updated = after_ref[block, :] + jnp.dot(
+            hidden, w_down_ref[...], preferred_element_type=F32
+        )
+        out_ref[block, :] = updated.astype(BF16)
+        copies.append(
+            pltpu.make_async_copy(out_ref.at[block], out_hbm.at[block], sems.at[part])
+        )
+        copies[-1].start()
+    for copy in copies:
+        copy.wait()
+
+
 def pick_kernel(flag_ref, yes_ref, no_ref, out_ref):
     first = yes_ref.shape[0] - out_ref.shape[0]
     out_ref[...] = jnp.where(
@@ -220,10 +258,10 @@
     if count & (count - 1):
         every = lax.all_gather(stats, axis)
         stats = joined([every[place] for place in range(count)], rows)
-        return stats[0], stats[1] / (count * rows)
+        return stats, stats, 2 * count * rows
     step = 1
-    while step < count:
-        if count % (16 * step) == 0 and step == 1:
+    while True:
+        if step == 1 and count % 16 == 0:
             stats = joined([stats, moved(stats, axis, lambda s: s ^ 1)], rows)
             side = lax.axis_index(axis) % 2
             last = moved(stats, axis, lambda s: s ^ 8)
@@ -232,12 +270,12 @@
                 for peer in (1, 2, 3)
             ]
             stats = joined([jnp.where(side == 0, stats, last)] + found, 2 * rows)
-            stats = joined([stats, moved(stats, axis, lambda s: s ^ 1)], 8 * rows)
-            step, rows = 16, 16 * rows
+            other, step, rows = moved(stats, axis, lambda s: s ^ 1), 16, 16 * rows
         else:
-            stats = joined([stats, moved(stats, axis, lambda s: s ^ step)], rows)
-            step, rows = 2 * step, 2 * rows
-    return stats[0], stats[1] / rows
+            other, step, rows = moved(stats, axis, lambda s: s ^ step), 2 * step, 2 * rows
+        if step >= count:
+            return stats, other, rows
+        stats = joined([stats, other], rows // 2)
 
 
 def body(
@@ -338,12 +376,17 @@
         cost_estimate=cost,
         name="attend_far1",
     )(far1, gain, w_key, w_value, query_heads, bias, sums, atoms, w_out)
-    mean, var = merged(stats, tile, "blk")
-    batched = ((after - mean) * lax.rsqrt(var + 1e-05) * bn_gain + bn_shift).astype(BF16)
-    hidden = jax.nn.gelu(
-        jnp.dot(batched, w_up, preferred_element_type=F32), approximate=True
-    ).astype(BF16)
-    return (after + jnp.dot(hidden, w_down, preferred_element_type=F32)).astype(BF16)
+    mine, other, count = merged(stats, tile, "blk")
+    return pl.pallas_call(
+        functools.partial(forward_kernel, count=count),
+        in_specs=[vmem] * 7,
+        out_specs=hbm,
+        out_shape=jax.ShapeDtypeStruct((tile, width), BF16),
+        scratch_shapes=[pltpu.VMEM((tile, width), BF16), pltpu.SemaphoreType.DMA((2,))],
+        compiler_params=params(12),
+        cost_estimate=cost,
+        name="feed_forward",
+    )(after, mine, other, bn_gain.reshape(1, width), bn_shift.reshape(1, width), w_up, w_down)
 
 
 def solution(mesh):

time: 81.5 us -> 81.5 us (level)
  matrix products: 2.25 us -> 0 us
  Pallas kernels: 46.8 us -> 48.9 us
    dot_general x1 -> x0, matrix products: 2.25 us -> none  [body(): jnp.dot(hidden, w_down, preferred_element_type=F32)]
    pallas_call x0 -> x1, Pallas kernels: none -> 2.14 us  [body(): pl.pallas_call(functools.partial(forward_kernel, count=count), in_specs=[...]
where the time goes in v3:
time: 81.5 us; the launch traced here: 81.4 us
  Pallas kernels  48.9 us (60%)
  starting transfers between devices  20.3 us (25%)
  waiting for transfers between devices  11.5 us (14%)
    pallas_call x4, Pallas kernels, body(): pl.pallas_call(functools.partial(next_kernel, slot=slot), in_specs=[vmem]...  28.3 us
    ppermute x11, starting transfers between devices, moved(): return lax.ppermute(value, axis, pairs)  20.3 us
    pallas_call x1, Pallas kernels, body(): pl.pallas_call(first_kernel, in_specs=[smem] + [hbm] * 6, out_specs=[vmem...  12.2 us
    ppermute x11, waiting for transfers between devices, moved(): return lax.ppermute(value, axis, pairs)  11.5 us
    pallas_call x1, Pallas kernels, body(): pl.pallas_call(functools.partial(last_kernel, slot=WIDTHS - 1, first=half...  6.24 us
    pallas_call x1, Pallas kernels, body(): pl.pallas_call(functools.partial(forward_kernel, count=count), in_specs=[...  2.14 us
  transfers between devices with their start and end apart: 11, of which 6 were waited for; matrix products, arithmetic and copies ran while one was open for 0% of the time, Pallas kernels for 50%

profile of v3, /device:TPU:0, one launch (start us, length us, event | category | flops | bytes accessed | tf_op | source)
XLA Modules:
  0.0 81.4 jit_solution(12368448348672445801)
XLA Ops:
  0.0 5.5 %collective-permute-start = (bf16[512,512]{1,0:T(8,128)(2,1)}, bf16[512,512]{1,0:T(8,128)(2,1)S(1)}, u32[]{:S(2)}, u32[]{:S(2)}) collective-permute-start(bf16[512,512]{1,0:T(8,128)(2,1)} %own_ref.1), channel_id=1, source_target_pairs={{0,15},{1,2},{2,1},{3,4},{4,3},{5,6},{6,5},{7,8},{8,7},{9,10},{10,... | collective-permute-start | bytes 1572872 | tf_op jit(solution)/shard_map/ppermute | solution.py:31
  5.5 0.0 collective-permute-start.4
  5.5 7.2 %collective-permute-done.yes_ref.rows_ref = bf16[512,512]{1,0:T(8,128)(2,1)S(1)} collective-permute-done((bf16[512,512]{1,0:T(8,128)(2,1)}, bf16[512,512]{1,0:T(8,128)(2,1)S(1)}, u32[]{:S(2)}, u32[]{:S(2)}) %collective-permute-start) | collective-permute-done | bytes 524320 | tf_op jit(solution)/shard_map/ppermute | solution.py:31
  12.6 3.2 %collective-permute-start.3 = (bf16[512,512]{1,0:T(8,128)(2,1)S(1)}, bf16[512,512]{1,0:T(8,128)(2,1)S(1)}, u32[]{:S(2)}, u32[]{:S(2)}) collective-permute-start(bf16[512,512]{1,0:T(8,128)(2,1)S(1)} %collective-permute-done.yes_ref.rows_ref), channel_id=1, source_target_pairs={{0,1},{1,0},{2,3},{3,2},{4,5},{5,4},{6,7},{7,6},{8,9},{9,8},{10,11... | collective-permute-start | bytes 1572872 | tf_op jit(solution)/shard_map/ppermute | solution.py:31
  15.8 0.1 stack.33.which_ref
  15.9 12.2 %attend_own.1 = (bf16[8,128,512]{2,1,0:T(8,128)(2,1)S(1)}, f32[5,512,512]{2,1,0:T(8,128)S(1)}, f32[8,80,512]{2,1,0:T(8,128)S(1)}, bf16[256,512]{1,0:T(8,128)(2,1)S(1)}, s32[1,512]{1,0:T(1,128)S(1)}) custom-call(s32[6]{0:T(128)S(1)} %stack.33.which_ref, bf16[512,512]{1,0:T(8,128)(2,1)} %own_ref.1, s32[1,5,512,512]{3,2,1,0:T(8,128)} %mask_hbm.1, ...), custom_call_target="tpu_custom_call" | custom-call | flops 1073741824 | bytes 1048576 | tf_op jit(solution)/shard_map/attend_own/pallas_call | solution.py:315
  28.1 0.0 copy-start
  28.1 0.0 copy-start.1
  28.1 0.0 copy-start.4
  28.1 1.7 %collective-permute-start.2 = (bf16[256,512]{1,0:T(8,128)(2,1)S(1)}, bf16[256,512]{1,0:T(8,128)(2,1)S(1)}, u32[]{:S(2)}, u32[]{:S(2)}) collective-permute-start(bf16[256,512]{1,0:T(8,128)(2,1)S(1)} %get-tuple-element.15), channel_id=1, source_target_pairs={{0,2},{1,15},{2,4},{3,1},{4,6},{5,3},{6,8},{7,5},{8,10},{9,7},{10,... | collective-permute-start | bytes 786440 | tf_op jit(solution)/shard_map/ppermute | solution.py:31
  29.8 0.0 copy-done.2
  29.8 0.1 pick_far.1
  29.9 1.5 %collective-permute-start.1 = (bf16[256,512]{1,0:T(8,128)(2,1)S(1)}, bf16[256,512]{1,0:T(8,128)(2,1)S(1)}, u32[]{:S(2)}, u32[]{:S(2)}) collective-permute-start(bf16[256,512]{1,0:T(8,128)(2,1)S(1)} %pick_far.1), channel_id=1, source_target_pairs={{0,2},{1,4},{2,15},{3,1},{4,6},{5,8},{6,3},{7,5},{8,10},{9,12},{10... | collective-permute-start | bytes 786440 | tf_op jit(solution)/shard_map/ppermute | solution.py:31
  31.4 0.0 collective-permute-done.4.rows_ref
  31.4 0.0 copy-done
  31.4 0.0 copy-done.1
  31.4 0.0 copy-done.4
  31.4 7.7 %shard_map.109.sum_in = f32[8,80,512]{2,1,0:T(8,128)S(1)} custom-call(bf16[512,512]{1,0:T(8,128)(2,1)S(1)} %collective-permute-done.4.rows_ref, f32[1,512]{1,0:T(1,128)S(1)} %bitcast.9, bf16[512,512]{1,0:T(8,128)(2,1)S(1)} %copy-done, bf16[512,512]{1,0:T(8,128)(2,1)S(1)} %copy-done.1, bf16[8,128,512]{2,1,0:T(8,128)(2,1)S(1)} %get-tuple-element.13.query_ref, ...), custom_call_target="tpu_custom_call" | custom-call | flops 1073741824 | bytes 1048576 | tf_op jit(solution)/shard_map/pallas_call | solution.py:357
  39.1 7.9 %shard_map.110.sum_in = f32[8,80,512]{2,1,0:T(8,128)S(1)} custom-call(bf16[512,512]{1,0:T(8,128)(2,1)S(1)} %collective-permute-done.yes_ref.rows_ref, f32[1,512]{1,0:T(1,128)S(1)} %bitcast.10, bf16[512,512]{1,0:T(8,128)(2,1)S(1)} %copy-done, bf16[512,512]{1,0:T(8,128)(2,1)S(1)} %copy-done.1, bf16[8,128,512]{2,1,0:T(8,128)(2,1)S(1)} %get-tuple-element.13.query_ref, ...), custom_call_target="tpu_custom_call" | custom-call | flops 1073741824 | bytes 1048576 | tf_op jit(solution)/shard_map/pallas_call | solution.py:357
  46.9 0.0 collective-permute-done.3.rows_ref
  46.9 7.7 %shard_map.111.sum_in = f32[8,80,512]{2,1,0:T(8,128)S(1)} custom-call(bf16[512,512]{1,0:T(8,128)(2,1)S(1)} %collective-permute-done.3.rows_ref, f32[1,512]{1,0:T(1,128)S(1)} %bitcast.11, bf16[512,512]{1,0:T(8,128)(2,1)S(1)} %copy-done, bf16[512,512]{1,0:T(8,128)(2,1)S(1)} %copy-done.1, bf16[8,128,512]{2,1,0:T(8,128)(2,1)S(1)} %get-tuple-element.13.query_ref, ...), custom_call_target="tpu_custom_call" | custom-call | flops 1073741824 | bytes 1048576 | tf_op jit(solution)/shard_map/pallas_call | solution.py:357
  54.6 0.0 copy-start.3
  54.6 0.0 collective-permute-done.2.rows_ref
  54.6 5.1 %shard_map.112.sum_in = f32[8,80,512]{2,1,0:T(8,128)S(1)} custom-call(bf16[256,512]{1,0:T(8,128)(2,1)S(1)} %collective-permute-done.2.rows_ref, f32[1,512]{1,0:T(1,128)S(1)} %bitcast.12, bf16[512,512]{1,0:T(8,128)(2,1)S(1)} %copy-done, bf16[512,512]{1,0:T(8,128)(2,1)S(1)} %copy-done.1, bf16[8,128,512]{2,1,0:T(8,128)(2,1)S(1)} %get-tuple-element.13.query_ref, ...), custom_call_target="tpu_custom_call" | custom-call | flops 1073741824 | bytes 1048576 | tf_op jit(solution)/shard_map/pallas_call | solution.py:357
  59.7 0.0 copy-start.5
  59.7 0.0 copy-start.6
  59.8 0.0 copy-start.7
  59.8 0.0 copy-start.8
  59.8 0.0 collective-permute-done.1.rows_ref
  59.8 0.0 copy-done.3
  59.8 6.2 %attend_far1.1 = (f32[512,512]{1,0:T(8,128)S(1)}, f32[2,512]{1,0:T(2,128)S(1)}) custom-call(bf16[256,512]{1,0:T(8,128)(2,1)S(1)} %collective-permute-done.1.rows_ref, f32[1,512]{1,0:T(1,128)S(1)} %bitcast.13, bf16[512,512]{1,0:T(8,128)(2,1)S(1)} %copy-done, bf16[512,512]{1,0:T(8,128)(2,1)S(1)} %copy-done.1, ...), custom_call_target="tpu_custom_call" | custom-call | flops 1073741824 | bytes 1048576 | tf_op jit(solution)/shard_map/attend_far1/pallas_call | solution.py:366
  66.0 1.9 %collective-permute-start.5 = (f32[2,512]{1,0:T(2,128)S(1)}, f32[2,512]{1,0:T(2,128)S(1)}, u32[]{:S(2)}, u32[]{:S(2)}) collective-permute-start(f32[2,512]{1,0:T(2,128)S(1)} %get-tuple-element.18), channel_id=1, source_target_pairs={{0,1},{1,0},{2,3},{3,2},{4,5},{5,4},{6,7},{7,6},{8,9},{9,8},{10,11... | collective-permute-start | bytes 12296 | tf_op jit(solution)/shard_map/ppermute | solution.py:31
  68.0 0.8 %collective-permute-done.5 = f32[2,512]{1,0:T(2,128)S(1)} collective-permute-done((f32[2,512]{1,0:T(2,128)S(1)}, f32[2,512]{1,0:T(2,128)S(1)}, u32[]{:S(2)}, u32[]{:S(2)}) %collective-permute-start.5) | collective-permute-done | bytes 4128 | tf_op jit(solution)/shard_map/ppermute | solution.py:31
  68.8 1.1 %collective-permute-start.6 = (f32[2,512]{1,0:T(2,128)S(1)}, f32[2,512]{1,0:T(2,128)S(1)}, u32[]{:S(2)}, u32[]{:S(2)}) collective-permute-start(f32[2,512]{1,0:T(2,128)S(1)} %pad_maximum_fusion), channel_id=1, source_target_pairs={{0,8},{1,9},{2,10},{3,11},{4,12},{5,13},{6,14},{7,15},{8,0},{9,1},... | collective-permute-start | bytes 12296 | tf_op jit(solution)/shard_map/ppermute | solution.py:31
  69.9 0.8 collective-permute-start.7
  70.7 0.9 %collective-permute-start.8 = (f32[2,512]{1,0:T(2,128)S(1)}, f32[2,512]{1,0:T(2,128)S(1)}, u32[]{:S(2)}, u32[]{:S(2)}) collective-permute-start(f32[2,512]{1,0:T(2,128)S(1)} %pad_maximum_fusion), channel_id=1, source_target_pairs={{0,4},{1,13},{2,6},{3,15},{4,0},{5,9},{6,2},{7,11},{8,12},{9,5},{1... | collective-permute-start | bytes 12296 | tf_op jit(solution)/shard_map/ppermute | solution.py:31
  71.7 1.8 %collective-permute-start.9 = (f32[2,512]{1,0:T(2,128)S(1)}, f32[2,512]{1,0:T(2,128)S(1)}, u32[]{:S(2)}, u32[]{:S(2)}) collective-permute-start(f32[2,512]{1,0:T(2,128)S(1)} %pad_maximum_fusion), channel_id=1, source_target_pairs={{0,6},{1,15},{2,4},{3,13},{4,2},{5,11},{6,0},{7,9},{8,14},{9,7},{1... | collective-permute-start | bytes 12296 | tf_op jit(solution)/shard_map/ppermute | solution.py:31
  73.4 0.0 collective-permute-done.6
  73.4 0.1 collective-permute-done.7
  73.6 0.8 collective-permute-done.8
  74.3 1.8 %collective-permute-done.9 = f32[2,512]{1,0:T(2,128)S(1)} collective-permute-done((f32[2,512]{1,0:T(2,128)S(1)}, f32[2,512]{1,0:T(2,128)S(1)}, u32[]{:S(2)}, u32[]{:S(2)}) %collective-permute-start.9) | collective-permute-done | bytes 4128 | tf_op jit(solution)/shard_map/ppermute | solution.py:31
  76.2 2.0 %collective-permute-start.10 = (f32[2,512]{1,0:T(2,128)S(1)}, f32[2,512]{1,0:T(2,128)S(1)}, u32[]{:S(2)}, u32[]{:S(2)}) collective-permute-start(f32[2,512]{1,0:T(2,128)S(1)} %pad_maximum_fusion.1.mine_ref), channel_id=1, source_target_pairs={{0,1},{1,0},{2,3},{3,2},{4,5},{5,4},{6,7},{7,6},{8,9},{9,8},{10,11... | collective-permute-start | bytes 12296 | tf_op jit(solution)/shard_map/ppermute | solution.py:31
  78.2 0.8 %collective-permute-done.10.other_ref = f32[2,512]{1,0:T(2,128)S(1)} collective-permute-done((f32[2,512]{1,0:T(2,128)S(1)}, f32[2,512]{1,0:T(2,128)S(1)}, u32[]{:S(2)}, u32[]{:S(2)}) %collective-permute-start.10) | collective-permute-done | bytes 4128 | tf_op jit(solution)/shard_map/ppermute | solution.py:31
  79.0 0.0 copy-done.5
  79.0 0.0 copy-done.6
  79.1 0.0 copy-done.7
  79.1 0.0 copy-done.8
  79.1 2.1 %feed_forward.1 = bf16[512,512]{1,0:T(8,128)(2,1)} custom-call(f32[512,512]{1,0:T(8,128)S(1)} %get-tuple-element.17.after_ref, f32[2,512]{1,0:T(2,128)S(1)} %pad_maximum_fusion.1.mine_ref, f32[2,512]{1,0:T(2,128)S(1)} %collective-permute-done.10.other_ref, f32[1,512]{1,0:T(1,128)S(1)} %bitcast.14, f32[1,512]{1,0:T(1,128)S(1)} %bitcast.15, ...), custom_call_target="tpu_custom_call" | custom-call | flops 1073741824 | bytes 1048576 | tf_op jit(solution)/shard_map/feed_forward/pallas_call | solution.py:380
  (6 shorter events, 0.1 us)
Async XLA Ops:
  0.0 12.6 %collective-permute-start = (bf16[512,512]{1,0:T(8,128)(2,1)}, bf16[512,512]{1,0:T(8,128)(2,1)S(1)}, u32[]{:S(2)}, u32[]{:S(2)}) collective-permute-start(bf16[512,512]{1,0:T(8,128)(2,1)} %own_ref.1), channel_id=1, source_target_pairs={{0,15},{1,2},{2,1},{3,4},{4,3},{5,6},{6,5},{7,8},{8,7},{9,10},{10,... | collective-permute-start | bytes 1572872 | tf_op jit(solution)/shard_map/ppermute | solution.py:31
  5.5 25.9 %collective-permute-start.4 = (bf16[512,512]{1,0:T(8,128)(2,1)}, bf16[512,512]{1,0:T(8,128)(2,1)S(1)}, u32[]{:S(2)}, u32[]{:S(2)}) collective-permute-start(bf16[512,512]{1,0:T(8,128)(2,1)} %own_ref.1), channel_id=1, source_target_pairs={{0,1},{1,0},{2,3},{3,2},{4,5},{5,4},{6,7},{7,6},{8,9},{9,8},{10,11... | collective-permute-start | bytes 1572872 | tf_op jit(solution)/shard_map/ppermute | solution.py:31
  12.6 34.3 %collective-permute-start.3 = (bf16[512,512]{1,0:T(8,128)(2,1)S(1)}, bf16[512,512]{1,0:T(8,128)(2,1)S(1)}, u32[]{:S(2)}, u32[]{:S(2)}) collective-permute-start(bf16[512,512]{1,0:T(8,128)(2,1)S(1)} %collective-permute-done.yes_ref.rows_ref), channel_id=1, source_target_pairs={{0,1},{1,0},{2,3},{3,2},{4,5},{5,4},{6,7},{7,6},{8,9},{9,8},{10,11... | collective-permute-start | bytes 1572872 | tf_op jit(solution)/shard_map/ppermute | solution.py:31
  15.9 13.9 %copy-start.2 = (bf16[512,512]{1,0:T(8,128)(2,1)S(1)}, bf16[512,512]{1,0:T(8,128)(2,1)}, u32[]{:S(2)}) copy-start(bf16[512,512]{1,0:T(8,128)(2,1)} %own_ref.1) | copy-start | bytes 1572868
  28.1 3.3 %copy-start = (bf16[512,512]{1,0:T(8,128)(2,1)S(1)}, bf16[512,512]{1,0:T(8,128)(2,1)}, u32[]{:S(2)}) copy-start(bf16[512,512]{1,0:T(8,128)(2,1)} %w_key_ref.9) | copy-start | bytes 1572868
  28.1 3.3 %copy-start.1 = (bf16[512,512]{1,0:T(8,128)(2,1)S(1)}, bf16[512,512]{1,0:T(8,128)(2,1)}, u32[]{:S(2)}) copy-start(bf16[512,512]{1,0:T(8,128)(2,1)} %w_value_ref.9) | copy-start | bytes 1572868
  28.1 3.3 %copy-start.4 = (f32[512]{0:T(512)S(1)}, f32[512]{0:T(512)}, u32[]{:S(2)}) copy-start(f32[512]{0:T(512)} %param.13) | copy-start | bytes 6148
  28.1 26.5 %collective-permute-start.2 = (bf16[256,512]{1,0:T(8,128)(2,1)S(1)}, bf16[256,512]{1,0:T(8,128)(2,1)S(1)}, u32[]{:S(2)}, u32[]{:S(2)}) collective-permute-start(bf16[256,512]{1,0:T(8,128)(2,1)S(1)} %get-tuple-element.15), channel_id=1, source_target_pairs={{0,2},{1,15},{2,4},{3,1},{4,6},{5,3},{6,8},{7,5},{8,10},{9,7},{10,... | collective-permute-start | bytes 786440 | tf_op jit(solution)/shard_map/ppermute | solution.py:31
  29.9 29.9 %collective-permute-start.1 = (bf16[256,512]{1,0:T(8,128)(2,1)S(1)}, bf16[256,512]{1,0:T(8,128)(2,1)S(1)}, u32[]{:S(2)}, u32[]{:S(2)}) collective-permute-start(bf16[256,512]{1,0:T(8,128)(2,1)S(1)} %pick_far.1), channel_id=1, source_target_pairs={{0,2},{1,4},{2,15},{3,1},{4,6},{5,8},{6,3},{7,5},{8,10},{9,12},{10... | collective-permute-start | bytes 786440 | tf_op jit(solution)/shard_map/ppermute | solution.py:31
  54.6 5.2 %copy-start.3 = (bf16[512,512]{1,0:T(8,128)(2,1)S(1)}, bf16[512,512]{1,0:T(8,128)(2,1)}, u32[]{:S(2)}) copy-start(bf16[512,512]{1,0:T(8,128)(2,1)} %w_out_ref.1) | copy-start | bytes 1572868
  59.7 19.3 %copy-start.5 = (bf16[512,1024]{1,0:T(8,128)(2,1)S(1)}, bf16[512,1024]{1,0:T(8,128)(2,1)}, u32[]{:S(2)}) copy-start(bf16[512,1024]{1,0:T(8,128)(2,1)} %w_up_ref.1) | copy-start | bytes 3145732
  59.7 19.3 %copy-start.6 = (bf16[1024,512]{1,0:T(8,128)(2,1)S(1)}, bf16[1024,512]{1,0:T(8,128)(2,1)}, u32[]{:S(2)}) copy-start(bf16[1024,512]{1,0:T(8,128)(2,1)} %w_down_ref.1) | copy-start | bytes 3145732
  59.8 19.3 %copy-start.7 = (f32[512]{0:T(512)S(1)}, f32[512]{0:T(512)}, u32[]{:S(2)}) copy-start(f32[512]{0:T(512)} %param.18) | copy-start | bytes 6148
  59.8 19.3 %copy-start.8 = (f32[512]{0:T(512)S(1)}, f32[512]{0:T(512)}, u32[]{:S(2)}) copy-start(f32[512]{0:T(512)} %param.19) | copy-start | bytes 6148
  66.0 2.8 %collective-permute-start.5 = (f32[2,512]{1,0:T(2,128)S(1)}, f32[2,512]{1,0:T(2,128)S(1)}, u32[]{:S(2)}, u32[]{:S(2)}) collective-permute-start(f32[2,512]{1,0:T(2,128)S(1)} %get-tuple-element.18), channel_id=1, source_target_pairs={{0,1},{1,0},{2,3},{3,2},{4,5},{5,4},{6,7},{7,6},{8,9},{9,8},{10,11... | collective-permute-start | bytes 12296 | tf_op jit(solution)/shard_map/ppermute | solution.py:31
  68.8 4.6 %collective-permute-start.6 = (f32[2,512]{1,0:T(2,128)S(1)}, f32[2,512]{1,0:T(2,128)S(1)}, u32[]{:S(2)}, u32[]{:S(2)}) collective-permute-start(f32[2,512]{1,0:T(2,128)S(1)} %pad_maximum_fusion), channel_id=1, source_target_pairs={{0,8},{1,9},{2,10},{3,11},{4,12},{5,13},{6,14},{7,15},{8,0},{9,1},... | collective-permute-start | bytes 12296 | tf_op jit(solution)/shard_map/ppermute | solution.py:31
  69.9 3.6 %collective-permute-start.7 = (f32[2,512]{1,0:T(2,128)S(1)}, f32[2,512]{1,0:T(2,128)S(1)}, u32[]{:S(2)}, u32[]{:S(2)}) collective-permute-start(f32[2,512]{1,0:T(2,128)S(1)} %pad_maximum_fusion), channel_id=1, source_target_pairs={{0,2},{1,11},{2,0},{3,9},{4,6},{5,15},{6,4},{7,13},{8,10},{9,3},{1... | collective-permute-start | bytes 12296 | tf_op jit(solution)/shard_map/ppermute | solution.py:31
  70.7 3.6 %collective-permute-start.8 = (f32[2,512]{1,0:T(2,128)S(1)}, f32[2,512]{1,0:T(2,128)S(1)}, u32[]{:S(2)}, u32[]{:S(2)}) collective-permute-start(f32[2,512]{1,0:T(2,128)S(1)} %pad_maximum_fusion), channel_id=1, source_target_pairs={{0,4},{1,13},{2,6},{3,15},{4,0},{5,9},{6,2},{7,11},{8,12},{9,5},{1... | collective-permute-start | bytes 12296 | tf_op jit(solution)/shard_map/ppermute | solution.py:31
  71.7 4.5 %collective-permute-start.9 = (f32[2,512]{1,0:T(2,128)S(1)}, f32[2,512]{1,0:T(2,128)S(1)}, u32[]{:S(2)}, u32[]{:S(2)}) collective-permute-start(f32[2,512]{1,0:T(2,128)S(1)} %pad_maximum_fusion), channel_id=1, source_target_pairs={{0,6},{1,15},{2,4},{3,13},{4,2},{5,11},{6,0},{7,9},{8,14},{9,7},{1... | collective-permute-start | bytes 12296 | tf_op jit(solution)/shard_map/ppermute | solution.py:31
  76.2 2.8 %collective-permute-start.10 = (f32[2,512]{1,0:T(2,128)S(1)}, f32[2,512]{1,0:T(2,128)S(1)}, u32[]{:S(2)}, u32[]{:S(2)}) collective-permute-start(f32[2,512]{1,0:T(2,128)S(1)} %pad_maximum_fusion.1.mine_ref), channel_id=1, source_target_pairs={{0,1},{1,0},{2,3},{3,2},{4,5},{5,4},{6,7},{7,6},{8,9},{9,8},{10,11... | collective-permute-start | bytes 12296 | tf_op jit(solution)/shard_map/ppermute | solution.py:31
